TPU v7x, 512 devices: a whole 4x4x16 slice. The times are simulated.
512 devices in a mesh: level: 8 (over y, core), slab: 64 (over x, z).
Axes of the slice: x: 4, y: 4, z: 16, core: 2. Of those that a mesh axis runs over, the one named last changes fastest.
Arguments:
- coef_fine: float32 [24, 512, 2048], P('level', 'slab'), may hold values from 0.2 to 5
- coef_coarse: float32 [24, 512, 2048], P('level', 'slab'), may hold values from 0.2 to 5
- rhs_field: float32 [512, 2048], P('slab'), may hold values from -6 to 6
- level_counts: int32 [8], P('level'), may hold values from 2 to 3, as said below
Outputs:
- solutions: float32 [24, 512, 2048], P('level', 'slab')
- sample_diffs: float32 [24], P('level')
- level_stats: float32 [8, 2], P('level')
- estimate: float32 [2], replicated
Inputs may be any that keep to these rules, and one draw needn't show every extreme that they name: `level_counts`: one level has exactly 3 live samples and another exactly 2.
All inputs are finite; a program needn't handle non-finite values.
Results may differ from a plain program's by a relative error of at most 0.0003.
Values sent between devices are 32-bit elements; how exact they have to be, the bound alone decides.
No kernel may reach another device: no remote copies, remote signals or barrier semaphores. Data moves between devices by JAX's collectives and lax.ppermute only.
A program may use at most 128 MiB of HBM per device.

v0:
```python
import functools

import jax
import jax.numpy as jnp
from jax import lax
from jax.experimental import pallas as pl
from jax.experimental.pallas import tpu as pltpu
from jax.sharding import Mesh
from jax.sharding import PartitionSpec as P

OMEGA = 0.8
SLAB = ("slab_0", "slab_1")
ROWS = 40
F32 = jnp.float32


def iota(shape, dim):
    return lax.broadcasted_iota(jnp.int32, shape, dim)


def right_of(x, cols):
    n = x.shape[1]
    return jnp.where(iota(x.shape, 1) == cols - 1, 0.0, pltpu.roll(x, n - 1, 1))


def below(x, period):
    n = x.shape[0]
    shifted = pltpu.roll(x, n - 1, 0)
    if period is None:
        return shifted
    return jnp.where(iota(x.shape, 0) % period == period - 1, 0.0, shifted)


def faces(k, cols, period):
    half = 0.5 * k
    first = iota(k.shape, 1) == 0
    fr = half + right_of(half, cols)
    fl = jnp.where(first, half, pltpu.roll(fr, 1, 1))
    fd = half + below(half, period)
    fu = pltpu.roll(fd, 1, 0)
    if period is not None:
        fu = jnp.where(iota(k.shape, 0) % period == 0, half, fu)
    return half, fr, fd, (fr + fl) + (fd + fu)


def fluxes(u, half, fr, fd, cols, period):
    q = fr * (u - right_of(u, cols))
    edge = -half * u
    ql = jnp.where(iota(u.shape, 1) == 0, edge, pltpu.roll(q, 1, 1))
    p = fd * (u - below(u, period))
    pu = pltpu.roll(p, 1, 0)
    if period is not None:
        pu = jnp.where(iota(u.shape, 0) % period == 0, edge, pu)
    return (q - ql) + (p - pu)


def pair_matrix(shape, dim, value):
    long, short = iota(shape, dim), iota(shape, 1 - dim)
    return jnp.where(long // 2 == short, value, 0.0).astype(F32)


def dot(a, b):
    return jnp.dot(a, b, precision=lax.Precision.HIGHEST, preferred_element_type=F32)


def pieces(x):
    return [x[:, i : i + 128] for i in range(0, x.shape[1], 128)]


def halve_rows(x, scratch):
    rows = x.shape[0]
    room = -(-rows // 16) * 16
    parts = pieces(x)
    for i, piece in enumerate(parts):
        scratch[i * room : i * room + rows, :] = piece
    out = room // 2
    got = scratch[pl.ds(0, len(parts) * out, stride=2), :] + scratch[pl.ds(1, len(parts) * out, stride=2), :]
    return jnp.concatenate([got[i * out : (i + 1) * out] for i in range(len(parts))], axis=1)


def halve_cols(xs, quarter):
    wide = 256 if xs[0].shape[1] >= 256 else 128
    n = xs[0].shape[1] // wide
    rows = [x.shape[0] for x in xs]
    tall = jnp.concatenate([x[:, i * wide : (i + 1) * wide] for x in xs for i in range(n)], axis=0)
    got = dot(tall, quarter[:wide])
    outs, at = [], 0
    for r in rows:
        outs.append(jnp.concatenate([got[at + i * r : at + (i + 1) * r] for i in range(n)], axis=1))
        at += n * r
    return outs


def double_cols(x, spread):
    n = max(x.shape[1] // 128, 1)
    rows = x.shape[0]
    tall = jnp.concatenate([x[:, i * 128 : (i + 1) * 128] for i in range(n)], axis=0)
    got = dot(tall, spread)
    return jnp.concatenate([got[i * rows : (i + 1) * rows] for i in range(n)], axis=1)


def double_rows(x, scratch, out_rows):
    rows = x.shape[0]
    parts = pieces(x)
    for i, piece in enumerate(parts):
        scratch[pl.ds(i * 2 * rows, rows, stride=2), :] = piece
        scratch[pl.ds(i * 2 * rows + 1, rows, stride=2), :] = piece
    return jnp.concatenate([scratch[i * 2 * rows : i * 2 * rows + out_rows, :] for i in range(len(parts))], axis=1)


def row_mask(shape, depth, edge_ref):
    row = iota(shape, 0)
    return (row >= (edge_ref[0] >> depth)) & (row < (edge_ref[1] >> depth))


def down_kernel(
    edge, kf, kc, g, kfu, kcu, gu, kfd, kcd, gd,
    packed, v0_out, v1_out, v2_out, s1_out, s2_out, k1_out, k2_out, to_below, to_above,
    scratch, parts,
):
    scratch[...] = jnp.zeros_like(scratch)
    quarter = pair_matrix((256, 128), 0, 0.25)
    slots = kf.shape[0]
    ncol = kf.shape[2]
    copies = packed.shape[0]
    source = jnp.concatenate([gu[...], g[...], gd[...]], axis=0)
    for i in range(copies):
        packed[i] = jnp.zeros(packed.shape[1:], F32)
    to_below[...] = jnp.zeros_like(to_below)
    to_above[...] = jnp.zeros_like(to_above)

    def one(slot, fine):
        field = slot if fine else slots + slot
        ku, ko, kd = (kfu, kf, kfd) if fine else (kcu, kc, kcd)
        k = jnp.concatenate([ku[slot], ko[slot], kd[slot]], axis=0)
        s, w = source, jnp.ones_like(source)
        total = jnp.zeros((8, 128), F32)
        for depth in range(3):
            rows, cols = k.shape
            own = 8 >> depth
            half, fr, fd, diag = faces(k, cols, None)
            inside = row_mask(k.shape, depth, edge)
            scale = jnp.where(inside, OMEGA / diag, 0.0)
            us, uw = scale * s, scale * w
            rs = s - fluxes(us, half, fr, fd, cols, None)
            rw = w - fluxes(uw, half, fr, fd, cols, None)
            share = rw * us + uw * s
            if depth == 0:
                share = share[8:16]
            else:
                row = iota(share.shape, 0)
                share = jnp.where((row >= own) & (row < 2 * own), share, 0.0)
            share = functools.reduce(jnp.add, [share[i : i + 8] for i in range(0, share.shape[0], 8)])
            share = functools.reduce(jnp.add, [share[:, i : i + 128] for i in range(0, cols, 128)])
            total = total + share * (16.0**depth)
            if fine:
                v = us * (4.0**depth)
                if depth == 0:
                    v0_out[slot] = v
                if depth == 1:
                    v1_out[slot], s1_out[slot], k1_out[slot] = v, s, k
                if depth == 2:
                    v2_out[slot], s2_out[slot], k2_out[slot] = v, s, k
                    to_below[pl.ds(slot, 1), :] = v[2:3]
                    to_above[pl.ds(slot, 1), :] = v[3:4]
            k, s, w = halve_cols([halve_rows(x, scratch) for x in (k, rs, rw)], quarter)
        for q, x in enumerate((k, s, w)):
            for half_at in range(2):
                line = x[1:2, half_at * 128 : (half_at + 1) * 128]
                for i in range(copies):
                    packed[i, pl.ds((q * 2 * slots + field) * 2 + half_at, 1), :] = line
        parts[pl.ds(field * 8, 8), :] = total

    def body(slot, _):
        one(slot, True)
        one(slot, False)
        return 0

    lax.fori_loop(0, slots, body, 0)
    lane = iota((1, 128), 1)
    line = jnp.zeros((1, 128), F32)
    for field in range(2 * slots):
        line = line + jnp.where(lane == field, jnp.sum(parts[field * 8 : field * 8 + 8]), 0.0)
    for i in range(copies):
        packed[i, 6 * slots * 2 : 6 * slots * 2 + 1, :] = line
    del ncol


def coarse_kernel(place, counts, gathered, e3, stats, message, scratch, whole, *, slots, slabs, cells):
    fields = 2 * slots
    quarter = pair_matrix((256, 128), 0, 0.25)
    spread = pair_matrix((128, 256), 1, 1.0)

    def taken(q):
        halves = [
            jnp.concatenate(
                [gathered[pl.ds((q * fields + f) * 2 + h, slabs, stride=ROWS), :] for f in range(fields)], axis=0
            )
            for h in range(2)
        ]
        return jnp.concatenate(halves, axis=1)

    def halved(xs):
        return halve_cols([halve_rows(x, scratch) for x in xs], quarter)

    k3, s3, w3 = taken(0), taken(1), taken(2)
    n = slabs
    half3, fr3, fd3, diag3 = faces(k3, 256, n)
    scale3 = OMEGA / diag3
    u3 = scale3 * s3
    k4, s4 = halved((k3, s3 - fluxes(u3, half3, fr3, fd3, 256, n)))
    half4, fr4, fd4, diag4 = faces(k4, 128, n // 2)
    scale4 = OMEGA / diag4
    u4 = scale4 * s4
    k5, s5 = halved((k4, s4 - fluxes(u4, half4, fr4, fd4, 128, n // 2)))
    half5, fr5, fd5, diag5 = faces(k5, 64, n // 4)
    scale5 = jnp.where(iota(diag5.shape, 1) < 64, OMEGA / diag5, 0.0)
    u5 = scale5 * s5
    for _ in range(3):
        u5 = u5 + scale5 * (s5 - fluxes(u5, half5, fr5, fd5, 64, n // 4))
    e4 = double_rows(double_cols(u5, spread[:, :128]), scratch, u4.shape[0])
    u4 = u4 + e4 * 4.0
    u4 = u4 + scale4 * (s4 - fluxes(u4, half4, fr4, fd4, 128, n // 2))
    u3 = u3 + double_rows(double_cols(u4, spread), scratch, u3.shape[0]) * 4.0
    u3 = u3 + scale3 * (s3 - fluxes(u3, half3, fr3, fd3, 256, n))
    v3 = u3 * 64.0

    lane = iota((1, 128), 1)
    quantity = jnp.sum(gathered[pl.ds(6 * fields, slabs, stride=ROWS), :], axis=0, keepdims=True)
    both = w3 * v3
    both = both[:, :128] + both[:, 128:]
    for f in range(fields):
        quantity = quantity + jnp.where(lane == f, 64.0 * jnp.sum(both[f * n : (f + 1) * n]), 0.0)
    quantity = quantity / cells
    diffs = jnp.where(lane < slots, quantity - pltpu.roll(quantity, 128 - slots, 1), 0.0)
    live = lane < counts[0]
    counted = counts[0].astype(F32)
    mean = jnp.sum(jnp.where(live, diffs, 0.0), axis=1, keepdims=True) / counted
    spare = jnp.where(live, diffs - mean, 0.0)
    var = jnp.sum(spare * spare, axis=1, keepdims=True) / jnp.maximum(counted - 1.0, 1.0)
    stats[...] = jnp.zeros_like(stats)
    stats[0:1, :] = diffs
    stats[1:2, :] = jnp.where(lane == 0, mean, jnp.where(lane == 1, var, 0.0))
    sent = jnp.where(lane == 0, mean, jnp.where(lane == 1, var / counted, 0.0))
    for i in range(message.shape[0]):
        message[i] = jnp.broadcast_to(sent, (8, 128))

    whole[...] = jnp.zeros_like(whole)
    whole[8 : 8 + slots * n, :] = v3[: slots * n]
    e3[...] = jnp.zeros_like(e3)
    me = place[0]
    for f in range(slots):
        for r in range(3):
            line = whole[pl.ds(8 + f * n + me + (r - 1), 1), :]
            if r == 0:
                line = jnp.where(me > 0, line, 0.0)
            if r == 2:
                line = jnp.where(me < n - 1, line, 0.0)
            e3[f * 8 + r : f * 8 + r + 1, :] = line


def up_kernel(edge, kf, kfu, kfd, g, v0, v1, v2, s1, s2, k1, k2, e3, above, below_rows, out, scratch):
    spread = pair_matrix((128, 256), 1, 1.0)
    slots = kf.shape[0]

    def body(slot, _):
        row = iota((8, v2.shape[2]), 0)
        v = jnp.where(row == 0, above[pl.ds(slot, 1), :], jnp.where(row == 5, below_rows[pl.ds(slot, 1), :], v2[slot]))
        e = e3[pl.ds(pl.multiple_of(slot * 8, 8), 8), :]
        zero = jnp.zeros_like(g[...])
        for depth, k, s, v in (
            (2, k2[slot], s2[slot], v),
            (1, k1[slot], s1[slot], v1[slot]),
            (0, jnp.concatenate([kfu[slot], kf[slot], kfd[slot]], axis=0), jnp.concatenate([zero, g[...], zero], axis=0), v0[slot]),
        ):
            rows, cols = k.shape
            inside = row_mask(k.shape, depth, edge)
            v = jnp.where(inside, v + double_rows(double_cols(e, spread), scratch, rows), 0.0)
            half, fr, fd, diag = faces(k, cols, None)
            e = v + OMEGA * (s * (4.0**depth) - fluxes(v, half, fr, fd, cols, None)) / diag
            e = jnp.where(inside, e, 0.0)
            if depth == 1:
                e = e[:16]
        out[slot] = e[8:16]
        return 0

    lax.fori_loop(0, slots, body, 0)


def sum_kernel(got, out):
    total = got[0]
    for i in range(1, got.shape[0]):
        total = total + got[i]
    out[...] = total


VMEM = pl.BlockSpec(memory_space=pltpu.VMEM)
SMEM = pl.BlockSpec(memory_space=pltpu.SMEM)


def shape(*dims):
    return jax.ShapeDtypeStruct(dims, F32)


def call(kernel, outs, smem, vmem, scratch, flops, name, mib):
    single = not isinstance(outs, (tuple, list))
    return pl.pallas_call(
        kernel,
        out_shape=outs,
        in_specs=[SMEM] * len(smem) + [VMEM] * len(vmem),
        out_specs=VMEM if single else [VMEM] * len(outs),
        scratch_shapes=scratch,
        compiler_params=pltpu.CompilerParams(vmem_limit_bytes=mib << 20),
        cost_estimate=pl.CostEstimate(flops=flops, bytes_accessed=1 << 20, transcendentals=0),
        name=name,
    )(*smem, *vmem)


def on_device(coef_fine, coef_coarse, rhs_field, level_counts):
    slots, rows, cols = coef_fine.shape
    fields = 2 * slots
    outer, inner = lax.axis_size("slab_0"), lax.axis_size("slab_1")
    levels = lax.axis_size("level")
    slabs = outer * inner
    me = lax.axis_index(SLAB)
    from_above = [(i, i + 1) for i in range(slabs - 1)]
    from_below = [(i + 1, i) for i in range(slabs - 1)]
    kfu = lax.ppermute(coef_fine, SLAB, from_above)
    kfd = lax.ppermute(coef_fine, SLAB, from_below)
    gu = lax.ppermute(rhs_field, SLAB, from_above)
    gd = lax.ppermute(rhs_field, SLAB, from_below)
    kcu = lax.ppermute(coef_coarse, SLAB, from_above)
    kcd = lax.ppermute(coef_coarse, SLAB, from_below)
    edge = jnp.stack([jnp.where(me == 0, 8, 0), jnp.where(me == slabs - 1, 16, 24)]).astype(jnp.int32)
    place = me.astype(jnp.int32).reshape(1)

    packed, v0, v1, v2, s1, s2, k1, k2, to_below, to_above = call(
        down_kernel,
        [
            shape(inner, ROWS, 128),
            shape(slots, 24, cols),
            shape(slots, 16, cols // 2),
            shape(slots, 8, cols // 4),
            shape(slots, 16, cols // 2),
            shape(slots, 8, cols // 4),
            shape(slots, 16, cols // 2),
            shape(slots, 8, cols // 4),
            shape(8, cols // 4),
            shape(8, cols // 4),
        ],
        [edge],
        [coef_fine, coef_coarse, rhs_field, kfu, kcu, gu, kfd, kcd, gd],
        [pltpu.VMEM((cols // 4, 128), F32), pltpu.VMEM((fields * 8, 128), F32)],
        20_000_000,
        "down",
        24,
    )
    lines = lax.all_to_all(packed, "slab_1", 0, 0, tiled=True)
    above = lax.ppermute(to_below, SLAB, from_above)
    below_rows = lax.ppermute(to_above, SLAB, from_below)
    wide = jnp.broadcast_to(lines.reshape(1, inner * ROWS, 128), (outer, inner * ROWS, 128))
    gathered = lax.all_to_all(wide, "slab_0", 0, 0, tiled=True).reshape(slabs * ROWS, 128)
    e3, stats, message = call(
        functools.partial(coarse_kernel, slots=slots, slabs=slabs, cells=float(rows * slabs * cols)),
        [shape(slots * 8, 256), shape(8, 128), shape(levels, 8, 128)],
        [place, level_counts],
        [gathered],
        [pltpu.VMEM((2 * fields * slabs, 128), F32), pltpu.VMEM((slots * slabs + 16, 256), F32)],
        5_000_000,
        "coarse",
        16,
    )
    got = lax.all_to_all(message, "level", 0, 0, tiled=True)
    solutions = call(
        up_kernel,
        shape(slots, rows, cols),
        [edge],
        [coef_fine, kfu, kfd, rhs_field, v0, v1, v2, s1, s2, k1, k2, e3, above, below_rows],
        [pltpu.VMEM((cols // 4, 128), F32)],
        10_000_000,
        "up",
        24,
    )
    total = call(sum_kernel, shape(8, 128), [], [got], [], 1_000, "total", 4)
    return solutions, stats[0, :slots], stats[1:2, :2], total[0, :2]


def solution(mesh):
    slabs = mesh.shape["slab"]
    outer = 4 if slabs >= 64 else 2
    split = Mesh(mesh.devices.reshape(mesh.shape["level"], outer, slabs // outer), ("level", "slab_0", "slab_1"))
    in_specs = (P("level", SLAB, None), P("level", SLAB, None), P(SLAB, None), P("level"))
    out_specs = (P("level", SLAB, None), P("level"), P("level", None), P())
    return jax.shard_map(on_device, mesh=split, in_specs=in_specs, out_specs=out_specs, check_vma=False)
```

profile of v0, /device:TPU:1, one launch (start us, length us, event | category | flops | bytes accessed | tf_op | source)
XLA Modules:
  0.0 112.2 jit_solution(9259352198806119817)
XLA Ops:
  0.6 4.4 %collective-permute-start = (f32[3,8,2048]{2,1,0:T(8,128)}, f32[3,8,2048]{2,1,0:T(8,128)S(1)}, u32[]{:S(2)}, u32[]{:S(2)}) collective-permute-start(f32[3,8,2048]{2,1,0:T(8,128)} %kf.3), channel_id=1, source_target_pairs={{0,1},{1,2},{2,3},{3,4},{4,5},{5,6},{6,7},{7,8},{8,9},{9,10},{10,1... | collective-permute-start | bytes 589832 | tf_op jit(solution)/shard_map/ppermute | solution.py:328
  5.0 1.3 %collective-permute-start.1 = (f32[3,8,2048]{2,1,0:T(8,128)}, f32[3,8,2048]{2,1,0:T(8,128)S(1)}, u32[]{:S(2)}, u32[]{:S(2)}) collective-permute-start(f32[3,8,2048]{2,1,0:T(8,128)} %kf.3), channel_id=1, source_target_pairs={{1,0},{2,1},{3,2},{4,3},{5,4},{6,5},{7,6},{8,7},{9,8},{10,9},{11,1... | collective-permute-start | bytes 589832 | tf_op jit(solution)/shard_map/ppermute | solution.py:329
  6.3 4.2 %collective-permute-start.2 = (f32[3,8,2048]{2,1,0:T(8,128)}, f32[3,8,2048]{2,1,0:T(8,128)S(1)}, u32[]{:S(2)}, u32[]{:S(2)}) collective-permute-start(f32[3,8,2048]{2,1,0:T(8,128)} %kc.1), channel_id=1, source_target_pairs={{0,1},{1,2},{2,3},{3,4},{4,5},{5,6},{6,7},{7,8},{8,9},{9,10},{10,1... | collective-permute-start | bytes 589832 | tf_op jit(solution)/shard_map/ppermute | solution.py:332
  10.5 1.3 %collective-permute-start.4 = (f32[3,8,2048]{2,1,0:T(8,128)}, f32[3,8,2048]{2,1,0:T(8,128)S(1)}, u32[]{:S(2)}, u32[]{:S(2)}) collective-permute-start(f32[3,8,2048]{2,1,0:T(8,128)} %kc.1), channel_id=1, source_target_pairs={{1,0},{2,1},{3,2},{4,3},{5,4},{6,5},{7,6},{8,7},{9,8},{10,9},{11,1... | collective-permute-start | bytes 589832 | tf_op jit(solution)/shard_map/ppermute | solution.py:333
  11.8 4.2 %collective-permute-start.3 = (f32[8,2048]{1,0:T(8,128)}, f32[8,2048]{1,0:T(8,128)S(1)}, u32[]{:S(2)}, u32[]{:S(2)}) collective-permute-start(f32[8,2048]{1,0:T(8,128)} %g.3), channel_id=1, source_target_pairs={{0,1},{1,2},{2,3},{3,4},{4,5},{5,6},{6,7},{7,8},{8,9},{9,10},{10,1... | collective-permute-start | bytes 196616 | tf_op jit(solution)/shard_map/ppermute | solution.py:330
  16.0 2.2 %collective-permute-done.3.gu = f32[8,2048]{1,0:T(8,128)S(1)} collective-permute-done((f32[8,2048]{1,0:T(8,128)}, f32[8,2048]{1,0:T(8,128)S(1)}, u32[]{:S(2)}, u32[]{:S(2)}) %collective-permute-start.3) | collective-permute-done | bytes 65568 | tf_op jit(solution)/shard_map/ppermute | solution.py:330
  18.2 1.3 %collective-permute-start.5 = (f32[8,2048]{1,0:T(8,128)}, f32[8,2048]{1,0:T(8,128)S(1)}, u32[]{:S(2)}, u32[]{:S(2)}) collective-permute-start(f32[8,2048]{1,0:T(8,128)} %g.3), channel_id=1, source_target_pairs={{1,0},{2,1},{3,2},{4,3},{5,4},{6,5},{7,6},{8,7},{9,8},{10,9},{11,1... | collective-permute-start | bytes 196616 | tf_op jit(solution)/shard_map/ppermute | solution.py:331
  19.5 0.1 pad_add_fusion.edge
  19.5 4.7 %collective-permute-done.5.gd = f32[8,2048]{1,0:T(8,128)S(1)} collective-permute-done((f32[8,2048]{1,0:T(8,128)}, f32[8,2048]{1,0:T(8,128)S(1)}, u32[]{:S(2)}, u32[]{:S(2)}) %collective-permute-start.5) | collective-permute-done | bytes 65568 | tf_op jit(solution)/shard_map/ppermute | solution.py:331
  24.2 0.0 collective-permute-done.kfu
  24.2 0.0 collective-permute-done.1.kfd
  24.2 0.0 collective-permute-done.2.kcu
  24.2 0.0 collective-permute-done.4.kcd
  24.2 0.0 copy-start
  24.2 0.9 copy-done
  25.2 0.0 copy-start.2
  25.2 0.8 copy-done.2
  26.0 0.0 copy-start.4
  26.0 0.9 copy-done.4
  26.9 13.1 %down.1 = (f32[16,40,128]{2,1,0:T(8,128)S(1)}, f32[3,24,2048]{2,1,0:T(8,128)S(1)}, f32[3,16,1024]{2,1,0:T(8,128)S(1)}, f32[3,8,512]{2,1,0:T(8,128)S(1)}, f32[3,1...) custom-call(s32[2]{0:T(128)S(1)} %pad_add_fusion.edge, ...), custom_call_target="tpu_custom_call" | custom-call | flops 20000000 | bytes 1048576 | tf_op jit(solution)/shard_map/down/pallas_call | solution.py:307
  40.1 30.0 %all_to_all.15 = f32[16,40,128]{2,1,0:T(8,128)S(1)} all-to-all(f32[16,40,128]{2,1,0:T(8,128)S(1)} %get-tuple-element.24), channel_id=1, replica_groups=mesh['level'=8,'slab_0'=4,'slab_1'=16] {'slab_1'}, dimensions={0} | all-to-all | bytes 655360 | tf_op jit(solution)/shard_map/all_to_all | solution.py:358
  70.0 1.2 %broadcast_in_dim.8 = f32[4,640,128]{2,1,0:T(8,128)} broadcast(f32[640,128]{1,0:T(8,128)S(1)} %bitcast.10), dimensions={1,2} | broadcast | bytes 1638400 | tf_op jit(solution)/shard_map/broadcast_in_dim | solution.py:361
  71.2 4.0 %all-to-all-start.1 = ((f32[4,640,128]{2,1,0:T(8,128)}), f32[4,640,128]{2,1,0:T(8,128)S(1)}, u32[]{:S(2)}, u32[]{:S(2)}) async-start(f32[4,640,128]{2,1,0:T(8,128)} %broadcast_in_dim.8), calls=%async_computation.1 | async-start | bytes 2621440 | tf_op jit(solution)/shard_map/all_to_all | solution.py:362
  75.2 0.0 copy-start.1
  75.2 0.0 copy-start.3
  75.9 6.1 %collective-permute-start.6 = (f32[8,512]{1,0:T(8,128)S(1)}, f32[8,512]{1,0:T(8,128)S(1)}, u32[]{:S(2)}, u32[]{:S(2)}) collective-permute-start(f32[8,512]{1,0:T(8,128)S(1)} %get-tuple-element.26), channel_id=1, source_target_pairs={{0,1},{1,2},{2,3},{3,4},{4,5},{5,6},{6,7},{7,8},{8,9},{9,10},{10,1... | collective-permute-start | bytes 49160 | tf_op jit(solution)/shard_map/ppermute | solution.py:359
  82.0 1.3 %collective-permute-start.7 = (f32[8,512]{1,0:T(8,128)S(1)}, f32[8,512]{1,0:T(8,128)S(1)}, u32[]{:S(2)}, u32[]{:S(2)}) collective-permute-start(f32[8,512]{1,0:T(8,128)S(1)} %get-tuple-element.27), channel_id=1, source_target_pairs={{1,0},{2,1},{3,2},{4,3},{5,4},{6,5},{7,6},{8,7},{9,8},{10,9},{11,1... | collective-permute-start | bytes 49160 | tf_op jit(solution)/shard_map/ppermute | solution.py:360
  83.3 3.2 %all-to-all-done.1 = f32[4,640,128]{2,1,0:T(8,128)S(1)} async-done(((f32[4,640,128]{2,1,0:T(8,128)}), f32[4,640,128]{2,1,0:T(8,128)S(1)}, u32[]{:S(2)}, u32[]{:S(2)}) %all-to-all-start.1) | async-done | bytes 1310752 | tf_op jit(solution)/shard_map/all_to_all | solution.py:362
  86.6 4.6 %coarse.1 = (f32[24,256]{1,0:T(8,128)S(1)}, f32[8,128]{1,0:T(8,128)S(1)}, f32[8,8,128]{2,1,0:T(8,128)}) custom-call(s32[1]{0:T(128)} %bitcast.2.place, s32[1]{0:T(128)S(6)} %copy.8.counts, f32[2560,128]{1,0:T(8,128)S(1)} %bitcast.9), custom_call_target="tpu_custom_call" | custom-call | flops 5000000 | bytes 1048576 | tf_op jit(solution)/shard_map/coarse/pallas_call | solution.py:307
  91.2 14.8 %all-to-all-start.2 = ((f32[8,8,128]{2,1,0:T(8,128)}), f32[8,8,128]{2,1,0:T(8,128)S(1)}, u32[]{:S(2)}, u32[]{:S(2)}) async-start(f32[8,8,128]{2,1,0:T(8,128)} %get-tuple-element.29), calls=%async_computation.2 | async-start | bytes 65536 | tf_op jit(solution)/shard_map/all_to_all | solution.py:373
  106.0 0.5 slice_bitcast_fusion.1
  106.5 0.5 slice.10
  107.0 0.0 collective-permute-done.6.above
  107.0 0.0 collective-permute-done.7.below_rows
  107.0 0.0 copy-done.1
  107.0 0.0 copy-done.3
  107.0 4.7 %up.1 = f32[3,8,2048]{2,1,0:T(8,128)} custom-call(s32[2]{0:T(128)S(1)} %pad_add_fusion.edge, f32[3,8,2048]{2,1,0:T(8,128)S(1)} %copy-done.1, f32[3,8,2048]{2,1,0:T(8,128)S(1)} %collective-permute-done.kfu, f32[3,8,2048]{2,1,0:T(8,128)S(1)} %collective-permute-done.1.kfd, f32[8,2048]{1,0:T(8,128)S(1)} %copy-done.3, f32[3,24,2048]{2,1,0:T(8,128)S(1)} %get-tuple-element.17.v0, ...), custom_call_target="tpu_custom_call" | custom-call | flops 10000000 | bytes 1048576 | tf_op jit(solution)/shard_map/up/pallas_call | solution.py:307
  111.7 0.0 all-to-all-done.2.got
  111.7 0.5 slice_bitcast_fusion
  (1 shorter events, 0.0 us)
Async XLA Ops:
  0.6 23.6 %collective-permute-start = (f32[3,8,2048]{2,1,0:T(8,128)}, f32[3,8,2048]{2,1,0:T(8,128)S(1)}, u32[]{:S(2)}, u32[]{:S(2)}) collective-permute-start(f32[3,8,2048]{2,1,0:T(8,128)} %kf.3), channel_id=1, source_target_pairs={{0,1},{1,2},{2,3},{3,4},{4,5},{5,6},{6,7},{7,8},{8,9},{9,10},{10,1... | collective-permute-start | bytes 589832 | tf_op jit(solution)/shard_map/ppermute | solution.py:328
  5.0 19.2 %collective-permute-start.1 = (f32[3,8,2048]{2,1,0:T(8,128)}, f32[3,8,2048]{2,1,0:T(8,128)S(1)}, u32[]{:S(2)}, u32[]{:S(2)}) collective-permute-start(f32[3,8,2048]{2,1,0:T(8,128)} %kf.3), channel_id=1, source_target_pairs={{1,0},{2,1},{3,2},{4,3},{5,4},{6,5},{7,6},{8,7},{9,8},{10,9},{11,1... | collective-permute-start | bytes 589832 | tf_op jit(solution)/shard_map/ppermute | solution.py:329
  6.3 17.9 %collective-permute-start.2 = (f32[3,8,2048]{2,1,0:T(8,128)}, f32[3,8,2048]{2,1,0:T(8,128)S(1)}, u32[]{:S(2)}, u32[]{:S(2)}) collective-permute-start(f32[3,8,2048]{2,1,0:T(8,128)} %kc.1), channel_id=1, source_target_pairs={{0,1},{1,2},{2,3},{3,4},{4,5},{5,6},{6,7},{7,8},{8,9},{9,10},{10,1... | collective-permute-start | bytes 589832 | tf_op jit(solution)/shard_map/ppermute | solution.py:332
  10.5 13.7 %collective-permute-start.4 = (f32[3,8,2048]{2,1,0:T(8,128)}, f32[3,8,2048]{2,1,0:T(8,128)S(1)}, u32[]{:S(2)}, u32[]{:S(2)}) collective-permute-start(f32[3,8,2048]{2,1,0:T(8,128)} %kc.1), channel_id=1, source_target_pairs={{1,0},{2,1},{3,2},{4,3},{5,4},{6,5},{7,6},{8,7},{9,8},{10,9},{11,1... | collective-permute-start | bytes 589832 | tf_op jit(solution)/shard_map/ppermute | solution.py:333
  11.8 6.4 %collective-permute-start.3 = (f32[8,2048]{1,0:T(8,128)}, f32[8,2048]{1,0:T(8,128)S(1)}, u32[]{:S(2)}, u32[]{:S(2)}) collective-permute-start(f32[8,2048]{1,0:T(8,128)} %g.3), channel_id=1, source_target_pairs={{0,1},{1,2},{2,3},{3,4},{4,5},{5,6},{6,7},{7,8},{8,9},{9,10},{10,1... | collective-permute-start | bytes 196616 | tf_op jit(solution)/shard_map/ppermute | solution.py:330
  18.2 6.0 %collective-permute-start.5 = (f32[8,2048]{1,0:T(8,128)}, f32[8,2048]{1,0:T(8,128)S(1)}, u32[]{:S(2)}, u32[]{:S(2)}) collective-permute-start(f32[8,2048]{1,0:T(8,128)} %g.3), channel_id=1, source_target_pairs={{1,0},{2,1},{3,2},{4,3},{5,4},{6,5},{7,6},{8,7},{9,8},{10,9},{11,1... | collective-permute-start | bytes 196616 | tf_op jit(solution)/shard_map/ppermute | solution.py:331
  24.2 0.9 copy-start
  25.2 0.8 copy-start.2
  26.0 0.9 copy-start.4
  71.2 15.3 %all-to-all-start.1 = ((f32[4,640,128]{2,1,0:T(8,128)}), f32[4,640,128]{2,1,0:T(8,128)S(1)}, u32[]{:S(2)}, u32[]{:S(2)}) async-start(f32[4,640,128]{2,1,0:T(8,128)} %broadcast_in_dim.8), calls=%async_computation.1 | async-start | bytes 2621440 | tf_op jit(solution)/shard_map/all_to_all | solution.py:362
  75.2 31.8 %copy-start.1 = (f32[3,8,2048]{2,1,0:T(8,128)S(1)}, f32[3,8,2048]{2,1,0:T(8,128)}, u32[]{:S(2)}) copy-start(f32[3,8,2048]{2,1,0:T(8,128)} %kf.3) | copy-start | bytes 589828
  75.2 31.8 %copy-start.3 = (f32[8,2048]{1,0:T(8,128)S(1)}, f32[8,2048]{1,0:T(8,128)}, u32[]{:S(2)}) copy-start(f32[8,2048]{1,0:T(8,128)} %g.3) | copy-start | bytes 196612
  75.9 31.1 %collective-permute-start.6 = (f32[8,512]{1,0:T(8,128)S(1)}, f32[8,512]{1,0:T(8,128)S(1)}, u32[]{:S(2)}, u32[]{:S(2)}) collective-permute-start(f32[8,512]{1,0:T(8,128)S(1)} %get-tuple-element.26), channel_id=1, source_target_pairs={{0,1},{1,2},{2,3},{3,4},{4,5},{5,6},{6,7},{7,8},{8,9},{9,10},{10,1... | collective-permute-start | bytes 49160 | tf_op jit(solution)/shard_map/ppermute | solution.py:359
  82.0 24.9 %collective-permute-start.7 = (f32[8,512]{1,0:T(8,128)S(1)}, f32[8,512]{1,0:T(8,128)S(1)}, u32[]{:S(2)}, u32[]{:S(2)}) collective-permute-start(f32[8,512]{1,0:T(8,128)S(1)} %get-tuple-element.27), channel_id=1, source_target_pairs={{1,0},{2,1},{3,2},{4,3},{5,4},{6,5},{7,6},{8,7},{9,8},{10,9},{11,1... | collective-permute-start | bytes 49160 | tf_op jit(solution)/shard_map/ppermute | solution.py:360
  91.2 20.5 %all-to-all-start.2 = ((f32[8,8,128]{2,1,0:T(8,128)}), f32[8,8,128]{2,1,0:T(8,128)S(1)}, u32[]{:S(2)}, u32[]{:S(2)}) async-start(f32[8,8,128]{2,1,0:T(8,128)} %get-tuple-element.29), calls=%async_computation.2 | async-start | bytes 65536 | tf_op jit(solution)/shard_map/all_to_all | solution.py:373
where the time goes:
time: 113 us; the launch traced here: 112 us
  starting transfers between devices  42.8 us (38%)
  blocking collectives  30 us (27%)
  Pallas kernels  22.5 us (20%)
  waiting for transfers between devices  10.1 us (9%)
  local copies, waits for them, and re-layouts  5.41 us (5%)
  between operations  1.45 us (1%)
    all_to_all x1, blocking collectives, on_device(): lines = lax.all_to_all(packed, 'slab_1', 0, 0, tiled=True)  30 us
    pallas_call x4, Pallas kernels, call(): pl.pallas_call(kernel, out_shape=outs, in_specs=[SMEM] * len(smem) + [VME...  22.5 us
    all_to_all x1, starting transfers between devices, on_device(): got = lax.all_to_all(message, 'level', 0, 0, tiled=True)  14.8 us
    ppermute x1, starting transfers between devices, on_device(): above = lax.ppermute(to_below, SLAB, from_above)  6.1 us
    ppermute x1, waiting for transfers between devices, on_device(): gd = lax.ppermute(rhs_field, SLAB, from_below)  4.66 us
    ppermute x1, starting transfers between devices, on_device(): kfu = lax.ppermute(coef_fine, SLAB, from_above)  4.37 us
    ppermute x1, starting transfers between devices, on_device(): kcu = lax.ppermute(coef_coarse, SLAB, from_above)  4.18 us
    ppermute x1, starting transfers between devices, on_device(): gu = lax.ppermute(rhs_field, SLAB, from_above)  4.17 us
  transfers between devices with their start and end apart: 10, of which 3 were waited for; matrix products, arithmetic and copies ran while one was open for 1% of the time, Pallas kernels for 8%

commit v1 on v0

v1 whole, which is shorter than its diff:
```python
import functools

import jax
import jax.numpy as jnp
from jax import lax
from jax.experimental import pallas as pl
from jax.experimental.pallas import tpu as pltpu
from jax.sharding import Mesh
from jax.sharding import PartitionSpec as P

OMEGA = 0.8
SLAB = ("slab_0", "slab_1")
LINES = 40
F32 = jnp.float32


def iota(shape, dim):
    return lax.broadcasted_iota(jnp.int32, shape, dim)


def right_of(x, cols):
    n = x.shape[1]
    return jnp.where(iota(x.shape, 1) == cols - 1, 0.0, pltpu.roll(x, n - 1, 1))


def below(x, period):
    n = x.shape[0]
    shifted = pltpu.roll(x, n - 1, 0)
    if period is None:
        return shifted
    return jnp.where(iota(x.shape, 0) % period == period - 1, 0.0, shifted)


def faces(k, cols, period):
    half = 0.5 * k
    first = iota(k.shape, 1) == 0
    fr = half + right_of(half, cols)
    fl = jnp.where(first, half, pltpu.roll(fr, 1, 1))
    fd = half + below(half, period)
    fu = pltpu.roll(fd, 1, 0)
    if period is not None:
        fu = jnp.where(iota(k.shape, 0) % period == 0, half, fu)
    return half, fr, fd, (fr + fl) + (fd + fu)


def across(u, half, fr, cols):
    q = fr * (u - right_of(u, cols))
    return q - jnp.where(iota(u.shape, 1) == 0, -half * u, pltpu.roll(q, 1, 1))


def fluxes(u, half, fr, fd, cols, period):
    p = fd * (u - below(u, period))
    pu = pltpu.roll(p, 1, 0)
    if period is not None:
        pu = jnp.where(iota(u.shape, 0) % period == 0, -half * u, pu)
    return across(u, half, fr, cols) + (p - pu)


def pair_matrix(shape, dim, value):
    long, short = iota(shape, dim), iota(shape, 1 - dim)
    return jnp.where(long // 2 == short, value, 0.0).astype(jnp.bfloat16)


def dot(a, b):
    high = a.astype(jnp.bfloat16)
    rest = a - high.astype(F32)
    middle = rest.astype(jnp.bfloat16)
    low = (rest - middle.astype(F32)).astype(jnp.bfloat16)
    one = functools.partial(jnp.dot, preferred_element_type=F32)
    return one(high, b) + (one(middle, b) + one(low, b))


def pieces(x, width=128):
    return [x[:, i : i + width] for i in range(0, x.shape[1], width)]


def pairs_of_rows(x, scratch):
    rows = x.shape[0]
    room = -(-rows // 16) * 16
    parts = pieces(x)
    for i, piece in enumerate(parts):
        scratch[i * room : i * room + rows, :] = piece
    out = len(parts) * room // 2
    return scratch[pl.ds(0, out, stride=2), :] + scratch[pl.ds(1, out, stride=2), :], room // 2


def halve(x, scratch, quarter):
    tall, rows = pairs_of_rows(x, scratch)
    n = x.shape[1] // 128
    blocks = [tall[i * rows : (i + 1) * rows] for i in range(n)]
    if n == 1:
        return dot(tall, quarter[:128])
    both = jnp.concatenate(
        [jnp.concatenate(blocks[0::2], axis=0), jnp.concatenate(blocks[1::2], axis=0)], axis=1
    )
    got = dot(both, quarter)
    return jnp.concatenate([got[i * rows : (i + 1) * rows] for i in range(n // 2)], axis=1)


def double_cols(x, spread):
    rows = x.shape[0]
    parts = pieces(x)
    got = dot(jnp.concatenate(parts, axis=0), spread)
    return jnp.concatenate([got[i * rows : (i + 1) * rows] for i in range(len(parts))], axis=1)


def double_rows(x, scratch):
    rows = x.shape[0]
    parts = pieces(x)
    for i, piece in enumerate(parts):
        scratch[pl.ds(i * 2 * rows, rows, stride=2), :] = piece
        scratch[pl.ds(i * 2 * rows + 1, rows, stride=2), :] = piece
    return jnp.concatenate([scratch[i * 2 * rows : (i + 1) * 2 * rows, :] for i in range(len(parts))], axis=1)


def inside(shape, depth, edge, window):
    row = iota(shape, 0) % window
    return (row >= (edge[0] >> depth)) & (row < (edge[1] >> depth))


def summed(parts):
    return functools.reduce(jnp.add, parts)


def sweep(k, s, w, depth, window, edge):
    cols = k.shape[1]
    half, fr, fd, diag = faces(k, cols, None)
    scale = jnp.where(inside(k.shape, depth, edge, window), OMEGA / diag, 0.0)
    us = scale * s
    uw = scale if w is None else scale * w
    rs = s - fluxes(us, half, fr, fd, cols, None)
    rw = (1.0 if w is None else w) - fluxes(uw, half, fr, fd, cols, None)
    return us, rs, rw, rw * us + uw * s


def down_kernel(
    edge, here, above, under,
    packed, rims, s1_out, s2_out, k1_out, k2_out, to_below, to_above,
    scratch, even, odd, parts,
):
    quarter = pair_matrix((256, 128), 0, 0.25)
    fields = here.shape[0] - 1
    slots = fields // 2
    copies = packed.shape[0]
    chunks = here.shape[2] // 128
    source = jnp.concatenate([above[fields], here[fields], under[fields]], axis=0)
    for q in range(3):
        for i in range(chunks):
            scratch[q, i * 32 + 24 : i * 32 + 32, :] = jnp.zeros((8, 128), F32)

    def finest(fine, field, _):
        k = jnp.concatenate([above[field], here[field], under[field]], axis=0)
        us, rs, rw, share = sweep(k, source, None, 0, 24, edge)
        parts[pl.ds(pl.multiple_of(field * 8, 8), 8), :] = summed(pieces(share[8:16]))
        if fine:
            rims[field, 0:1, :] = k[7:8]
            rims[field, 1:2, :] = k[16:17]
            rims[field, 2:3, :] = us[7:8]
            rims[field, 3:4, :] = us[16:17]
        for q, x in enumerate((k, rs, rw)):
            tall, rows = pairs_of_rows(x, scratch.at[q])
            for i in range(chunks):
                into = even if i % 2 == 0 else odd
                at = pl.multiple_of((q * (chunks // 2) + i // 2) * fields * rows + field * rows, 8)
                into[pl.ds(at, rows), :] = tall[i * rows : (i + 1) * rows]
        return 0

    lax.fori_loop(0, slots, functools.partial(finest, True), 0)
    lax.fori_loop(slots, fields, functools.partial(finest, False), 0)

    block = fields * 16
    level = []
    for q in range(3):
        span = slice(q * (chunks // 2) * block, (q + 1) * (chunks // 2) * block)
        got = dot(jnp.concatenate([even[span, :], odd[span, :]], axis=1), quarter)
        level.append(jnp.concatenate([got[i * block : (i + 1) * block] for i in range(chunks // 2)], axis=1))
    for depth, window in ((1, 16), (2, 8)):
        k, s, w = level
        us, rs, rw, share = sweep(k, s, w, depth, window, edge)
        own = 8 >> depth
        row = iota(share.shape, 0) % window
        share = summed(pieces(jnp.where((row >= own) & (row < 2 * own), share, 0.0))) * (16.0**depth)
        for field in range(fields):
            at = field * window
            parts[field * 8 : field * 8 + 8, :] += summed([share[at + i : at + i + 8] for i in range(0, window, 8)])
        kept = slots * window
        if depth == 1:
            s1_out[...], k1_out[...] = s[:kept], k[:kept]
        else:
            s2_out[...], k2_out[...] = s[:kept], k[:kept]
            to_below[...] = jnp.zeros_like(to_below)
            to_above[...] = jnp.zeros_like(to_above)
            for slot in range(slots):
                to_below[slot : slot + 1, :] = us[slot * 8 + 2 : slot * 8 + 3] * 16.0
                to_above[slot : slot + 1, :] = us[slot * 8 + 3 : slot * 8 + 4] * 16.0
        level = [halve(x, scratch.at[q], quarter) for q, x in enumerate((k, rs, rw))]

    for q, x in enumerate(level):
        for field in range(fields):
            for h in range(2):
                line = x[field * 4 + 1 : field * 4 + 2, h * 128 : (h + 1) * 128]
                packed[0, (q * fields + field) * 2 + h : (q * fields + field) * 2 + h + 1, :] = line
    lane = iota((1, 128), 1)
    line = jnp.zeros((1, 128), F32)
    for field in range(fields):
        line = line + jnp.where(lane == field, jnp.sum(parts[field * 8 : field * 8 + 8, :]), 0.0)
    packed[0, 6 * fields : 6 * fields + 1, :] = line
    packed[0, 6 * fields + 1 :, :] = jnp.zeros((LINES - 6 * fields - 1, 128), F32)
    for i in range(1, copies):
        packed[i] = packed[0]


def coarse_kernel(place, counts, gathered, lines, top, bottom, e3, message, scratch, whole, *, fields, slabs, rows, cells):
    del top, bottom
    slots = fields // 2
    quarter = pair_matrix((256, 128), 0, 0.25)
    spread = pair_matrix((128, 256), 1, 1.0)
    stride = 4 * fields
    n = slabs

    def taken(q):
        halves = [
            jnp.concatenate(
                [gathered[pl.ds((q * fields + f) * 2 + h, n, stride=stride), :] for f in range(fields)], axis=0
            )
            for h in range(2)
        ]
        return jnp.concatenate(halves, axis=1)

    k3, s3 = taken(0), taken(1)
    half3, fr3, fd3, diag3 = faces(k3, 256, n)
    scale3 = OMEGA / diag3
    u3 = scale3 * s3
    k4 = halve(k3, scratch.at[0], quarter)
    s4 = halve(s3 - fluxes(u3, half3, fr3, fd3, 256, n), scratch.at[1], quarter)
    half4, fr4, fd4, diag4 = faces(k4, 128, n // 2)
    scale4 = OMEGA / diag4
    u4 = scale4 * s4
    k5 = halve(k4, scratch.at[0], quarter)
    s5 = halve(s4 - fluxes(u4, half4, fr4, fd4, 128, n // 2), scratch.at[1], quarter)
    half5, fr5, fd5, diag5 = faces(k5, 64, n // 4)
    scale5 = jnp.where(iota(diag5.shape, 1) < 64, OMEGA / diag5, 0.0)
    u5 = scale5 * s5
    for _ in range(3):
        u5 = u5 + scale5 * (s5 - fluxes(u5, half5, fr5, fd5, 64, n // 4))
    u4 = u4 + double_rows(double_cols(u5, spread[:, :128]), scratch.at[0]) * 4.0
    u4 = u4 + scale4 * (s4 - fluxes(u4, half4, fr4, fd4, 128, n // 2))
    u3 = u3 + double_rows(double_cols(u4, spread), scratch.at[0]) * 4.0
    u3 = u3 + scale3 * (s3 - fluxes(u3, half3, fr3, fd3, 256, n))
    v3 = u3 * 64.0
    whole[0:8, :] = jnp.zeros((8, 256), F32)
    whole[8 : 8 + fields * n, :] = v3
    whole[8 + fields * n :, :] = jnp.zeros((8, 256), F32)

    lane = iota((1, 128), 1)
    block = pl.multiple_of(place[1] * rows, 8)

    def weighed(f):
        v = whole[pl.ds(8 + f * n + block, rows), :]
        w = [lines[pl.ds((2 * fields + f) * 2 + h, rows, stride=LINES), :] for h in range(2)]
        return v[:, :128] * w[0] + v[:, 128:] * w[1]

    total = jnp.sum(lines[pl.ds(6 * fields, rows, stride=LINES), :], axis=0, keepdims=True)
    total = total - pltpu.roll(total, 128 - slots, 1)
    for f in range(slots):
        total = total + jnp.where(lane == f, 64.0 * jnp.sum(weighed(f) - weighed(slots + f)), 0.0)
    sent = jnp.where(lane < slots, total / cells, jnp.where(lane == slots, counts[0].astype(F32), 0.0))
    sent = jnp.broadcast_to(sent, (8, 128))
    for i in range(message.shape[0]):
        message[i] = sent

    me = place[0]
    e3[...] = jnp.zeros_like(e3)
    for f in range(slots):
        for r in range(3):
            line = whole[pl.ds(8 + f * n + me + (r - 1), 1), :]
            if r == 0:
                line = jnp.where(me > 0, line, 0.0)
            if r == 2:
                line = jnp.where(me < n - 1, line, 0.0)
            e3[f * 8 + r : f * 8 + r + 1, :] = line


def up_kernel(edge, here, g, rims, s1, s2, k1, k2, e3, top, bottom, out, scratch):
    spread = pair_matrix((128, 256), 1, 1.0)
    slots = here.shape[0]

    def relaxed(k, s, e, depth, window, swap):
        half, fr, fd, diag = faces(k, k.shape[1], None)
        scale = OMEGA / diag
        s = s * (4.0**depth)
        valid = inside(k.shape, depth, edge, window)
        v = jnp.where(valid, swap(scale * s) + e, 0.0)
        return jnp.where(valid, v + scale * (s - fluxes(v, half, fr, fd, k.shape[1], None)), 0.0)

    def stacked(ref, rows):
        return jnp.concatenate([jnp.broadcast_to(ref[f : f + 1, :], (rows, ref.shape[1])) for f in range(slots)], axis=0)

    def rimmed(v):
        row = iota(v.shape, 0) % 8
        return jnp.where(row == 0, stacked(top, 8), jnp.where(row == 5, stacked(bottom, 8), v))

    e = double_rows(double_cols(e3[...], spread), scratch)
    e = jnp.concatenate([e[f * 16 : f * 16 + 8] for f in range(slots)], axis=0)
    e = relaxed(k2[...], s2[...], e, 2, 8, rimmed)
    e = double_rows(double_cols(e, spread), scratch)
    e = relaxed(k1[...], s1[...], e, 1, 16, lambda v: v)
    e = double_cols(e, spread)
    g = g[...]
    row = iota(g.shape, 0)
    cols = g.shape[1]

    def lower(x, last):
        return jnp.where(row == 7, last, pltpu.roll(x, 7, 0))

    def upper(x, first):
        return jnp.where(row == 0, first, pltpu.roll(x, 1, 0))

    for f in range(slots):
        k = here[f]
        half = 0.5 * k
        fr = half + right_of(half, cols)
        fl = jnp.where(iota(k.shape, 1) == 0, half, pltpu.roll(fr, 1, 1))
        fd = half + lower(half, 0.5 * rims[f, 1:2, :])
        fu = half + upper(half, 0.5 * rims[f, 0:1, :])
        scale = OMEGA / ((fr + fl) + (fd + fu))
        at = f * 16
        v = scale * g + double_rows(e[at : at + 8], scratch)[8:16]
        first = rims[f, 2:3, :] + e[at + 3 : at + 4]
        last = rims[f, 3:4, :] + e[at + 8 : at + 9]
        flow = across(v, half, fr, cols) + (fd * (v - lower(v, last)) + fu * (v - upper(v, first)))
        out[f] = v + scale * (g - flow)


def final_kernel(place, got, diffs, moments, estimate, *, levels, outer):
    slots = diffs.shape[0]
    row, lane = iota((8, 128), 0), iota((8, 128), 1)
    table = jnp.zeros((8, 128), F32)
    for m in range(levels):
        table = jnp.where(row == m, summed([got[m * outer + i] for i in range(outer)]), table)

    def along(x):
        return jnp.sum(x, axis=1, keepdims=True)

    counted = along(jnp.where(lane == slots, table, 0.0)) / outer
    counted = jnp.where(row[:, :1] < levels, counted, 1.0)
    live = (lane < slots) & (lane.astype(F32) < counted) & (row < levels)
    mean = along(jnp.where(live, table, 0.0)) / counted
    spare = jnp.where(live, table - mean, 0.0)
    var = along(spare * spare) / jnp.maximum(counted - 1.0, 1.0)
    both = jnp.where(lane == 0, mean, jnp.where(lane == 1, var, 0.0))
    sums = jnp.where(lane == 0, mean, jnp.where(lane == 1, var / counted, 0.0))
    sums = jnp.sum(sums, axis=0, keepdims=True)
    mine = row == place[2]
    own = jnp.sum(jnp.where(mine, table, 0.0), axis=0, keepdims=True)
    both = jnp.sum(jnp.where(mine, both, 0.0), axis=0, keepdims=True)
    for i in range(slots):
        diffs[i] = own[0, i]
    for i in range(2):
        moments[0, i] = both[0, i]
        estimate[i] = sums[0, i]


VMEM = pl.BlockSpec(memory_space=pltpu.VMEM)
SMEM = pl.BlockSpec(memory_space=pltpu.SMEM)


def shape(*dims):
    return jax.ShapeDtypeStruct(dims, F32)


def call(kernel, outs, smem, vmem, scratch, flops, name, mib, scalars=0):
    return pl.pallas_call(
        kernel,
        out_shape=outs,
        in_specs=[SMEM] * len(smem) + [VMEM] * len(vmem),
        out_specs=[VMEM] * (len(outs) - scalars) + [SMEM] * scalars,
        scratch_shapes=[pltpu.VMEM(s, F32) for s in scratch],
        compiler_params=pltpu.CompilerParams(vmem_limit_bytes=mib << 20),
        cost_estimate=pl.CostEstimate(flops=flops, bytes_accessed=1 << 20, transcendentals=0),
        name=name,
    )(*smem, *vmem)


def on_device(coef_fine, coef_coarse, rhs_field, level_counts):
    slots, rows, cols = coef_fine.shape
    fields = 2 * slots
    outer, inner = lax.axis_size("slab_0"), lax.axis_size("slab_1")
    levels = lax.axis_size("level")
    slabs = outer * inner
    me = lax.axis_index(SLAB)
    from_above = [(i, i + 1) for i in range(slabs - 1)]
    from_below = [(i + 1, i) for i in range(slabs - 1)]
    here = jnp.concatenate([coef_fine, coef_coarse, rhs_field[None]], axis=0)
    above = lax.ppermute(here, SLAB, from_above)
    under = lax.ppermute(here, SLAB, from_below)
    edge = jnp.stack([jnp.where(me == 0, 8, 0), jnp.where(me == slabs - 1, 16, 24)]).astype(jnp.int32)
    place = jnp.stack([me, lax.axis_index("slab_0"), lax.axis_index("level")]).astype(jnp.int32)

    packed, rims, s1, s2, k1, k2, to_below, to_above = call(
        down_kernel,
        [
            shape(inner, LINES, 128),
            shape(slots, 8, cols),
            shape(slots * 16, cols // 2),
            shape(slots * 8, cols // 4),
            shape(slots * 16, cols // 2),
            shape(slots * 8, cols // 4),
            shape(8, cols // 4),
            shape(8, cols // 4),
        ],
        [edge],
        [here, above, under],
        [
            (3, max(cols // 4, 768), 128),
            (3 * fields * cols // 16, 128),
            (3 * fields * cols // 16, 128),
            (fields * 8, 128),
        ],
        20_000_000,
        "down",
        28,
    )
    lines = lax.all_to_all(packed, "slab_1", 0, 0, tiled=True)
    lines, to_below, to_above = lax.optimization_barrier((lines, to_below, to_above))
    top = lax.ppermute(to_below, SLAB, from_above)
    bottom = lax.ppermute(to_above, SLAB, from_below)
    used = 4 * fields
    wide = jnp.broadcast_to(lines[None, :, :used], (outer, inner, used, 128))
    gathered = lax.all_to_all(wide, "slab_0", 0, 0, tiled=True).reshape(slabs * used, 128)
    e3, message = call(
        functools.partial(coarse_kernel, fields=fields, slabs=slabs, rows=inner, cells=float(rows * slabs * cols)),
        [shape(slots * 8, 256), shape(levels * outer, 8, 128)],
        [place, level_counts],
        [gathered, lines.reshape(inner * LINES, 128), top, bottom],
        [(2, 2 * fields * slabs, 128), (fields * slabs + 16, 256)],
        5_000_000,
        "coarse",
        16,
    )
    got = lax.all_to_all(message, ("level", "slab_0"), 0, 0, tiled=True)
    (solutions,) = call(
        up_kernel,
        [shape(slots, rows, cols)],
        [edge],
        [coef_fine, rhs_field, rims, s1, s2, k1, k2, e3, top, bottom],
        [(cols // 2, 128)],
        10_000_000,
        "up",
        16,
    )
    diffs, moments, estimate = call(
        functools.partial(final_kernel, levels=levels, outer=outer),
        [shape(slots), shape(1, 2), shape(2)],
        [place],
        [got],
        [],
        1_000,
        "final",
        4,
        3,
    )
    return solutions, diffs, moments, estimate


def solution(mesh):
    slabs = mesh.shape["slab"]
    outer = 4 if slabs >= 64 else 2
    split = Mesh(mesh.devices.reshape(mesh.shape["level"], outer, slabs // outer), ("level", "slab_0", "slab_1"))
    in_specs = (P("level", SLAB, None), P("level", SLAB, None), P(SLAB, None), P("level"))
    out_specs = (P("level", SLAB, None), P("level"), P("level", None), P())
    return jax.shard_map(on_device, mesh=split, in_specs=in_specs, out_specs=out_specs, check_vma=False)
```

time: 113 us -> 97.9 us (0.87)
  starting transfers between devices: 42.8 us -> 32.4 us
  Pallas kernels: 22.5 us -> 14.6 us
  local copies, waits for them, and re-layouts: 5.41 us -> 0.96 us
  blocking collectives: 30 us -> 33.9 us
  waiting for transfers between devices: 10.1 us -> 13 us
  other arithmetic: 0.08 us -> 1.24 us
    ppermute x8 -> x4, starting transfers between devices: 24 us -> 15.9 us  [the longest x1 8.31 us: on_device(): top = lax.ppermute(to_below, SLAB, from_above)]
    pallas_call x4, Pallas kernels: 22.5 us -> 14.6 us  [call(): pl.pallas_call(kernel, out_shape=outs, in_specs=[SMEM] * len(smem) + [VME...]
    all_to_all x1, blocking collectives: 30 us -> 33.9 us  [on_device(): lines = lax.all_to_all(packed, 'slab_1', 0, 0, tiled=True)]
    unnamed x10 -> x4, local copies, waits for them, and re-layouts: 2.69 us -> 0.01 us
    all_to_all x2, starting transfers between devices: 18.8 us -> 16.5 us  [the longest x1 12.5 us: on_device(): got = lax.all_to_all(message, ('level', 'slab_0'), 0, 0, tiled=True)]
    all_to_all x2, waiting for transfers between devices: 3.22 us -> 4.99 us  [the longest x1 4.99 us: on_device(): got = lax.all_to_all(message, ('level', 'slab_0'), 0, 0, tiled=True)]
    ppermute x8 -> x4, waiting for transfers between devices: 6.87 us -> 8.02 us  [the longest x1 3.81 us: on_device(): under = lax.ppermute(here, SLAB, from_below)]
  transfers between devices with their start and end apart: 10 -> 6, of which waited for: 3 -> 4; matrix products, arithmetic and copies ran while one was open for 1% -> 0% of each run, Pallas kernels for 8% -> 3%
where the time goes in v1:
time: 97.9 us; the launch traced here: 97.6 us
  blocking collectives  33.9 us (35%)
  starting transfers between devices  32.4 us (33%)
  Pallas kernels  14.6 us (15%)
  waiting for transfers between devices  13 us (13%)
  between operations  1.38 us (1%)
  other arithmetic  1.24 us (1%)
    all_to_all x1, blocking collectives, on_device(): lines = lax.all_to_all(packed, 'slab_1', 0, 0, tiled=True)  33.9 us
    pallas_call x4, Pallas kernels, call(): pl.pallas_call(kernel, out_shape=outs, in_specs=[SMEM] * len(smem) + [VME...  14.6 us
    all_to_all x1, starting transfers between devices, on_device(): got = lax.all_to_all(message, ('level', 'slab_0'), 0, 0, tiled=True)  12.5 us
    ppermute x1, starting transfers between devices, on_device(): top = lax.ppermute(to_below, SLAB, from_above)  8.31 us
    ppermute x1, starting transfers between devices, on_device(): above = lax.ppermute(here, SLAB, from_above)  5.02 us
    all_to_all x1, waiting for transfers between devices, on_device(): got = lax.all_to_all(message, ('level', 'slab_0'), 0, 0, tiled=True)  4.99 us
    all_to_all x1, starting transfers between devices, on_device(): lax.all_to_all(wide, 'slab_0', 0, 0, tiled=True).reshape(slabs * used, 128)  4.03 us
    ppermute x1, waiting for transfers between devices, on_device(): under = lax.ppermute(here, SLAB, from_below)  3.81 us
  transfers between devices with their start and end apart: 6, of which 4 were waited for; matrix products, arithmetic and copies ran while one was open for 0% of the time, Pallas kernels for 3%

profile of v1, /device:TPU:1, one launch (start us, length us, event | category | flops | bytes accessed | tf_op | source)
XLA Modules:
  0.0 97.6 jit_solution(16603666420310383564)
XLA Ops:
  0.6 1.1 %pad_maximum_fusion.here = f32[7,8,2048]{2,1,0:T(8,128)S(1)} fusion(f32[1,8,2048]{2,1,0:T(8,128)} %bitcast.10, f32[3,8,2048]{2,1,0:T(8,128)} %param.5, f32[3,8,2048]{2,1,0:T(8,128)} %here.1), kind=kLoop, calls=%fused_computation | loop fusion | flops 229376 | bytes 917504 | tf_op jit(solution)/shard_map/concatenate | solution.py:394
  1.7 1.3 %collective-permute-start.1 = (f32[7,8,2048]{2,1,0:T(8,128)S(1)}, f32[7,8,2048]{2,1,0:T(8,128)S(1)}, u32[]{:S(2)}, u32[]{:S(2)}) collective-permute-start(f32[7,8,2048]{2,1,0:T(8,128)S(1)} %pad_maximum_fusion.here), channel_id=1, source_target_pairs={{1,0},{2,1},{3,2},{4,3},{5,4},{6,5},{7,6},{8,7},{9,8},{10,9},{11,1... | collective-permute-start | bytes 1376264 | tf_op jit(solution)/shard_map/ppermute | solution.py:396
  3.0 5.0 %collective-permute-start = (f32[7,8,2048]{2,1,0:T(8,128)S(1)}, f32[7,8,2048]{2,1,0:T(8,128)S(1)}, u32[]{:S(2)}, u32[]{:S(2)}) collective-permute-start(f32[7,8,2048]{2,1,0:T(8,128)S(1)} %pad_maximum_fusion.here), channel_id=1, source_target_pairs={{0,1},{1,2},{2,3},{3,4},{4,5},{5,6},{6,7},{7,8},{8,9},{9,10},{10,1... | collective-permute-start | bytes 1376264 | tf_op jit(solution)/shard_map/ppermute | solution.py:395
  8.1 0.1 pad_add_fusion.edge
  8.1 3.8 %collective-permute-done.1.under = f32[7,8,2048]{2,1,0:T(8,128)S(1)} collective-permute-done((f32[7,8,2048]{2,1,0:T(8,128)S(1)}, f32[7,8,2048]{2,1,0:T(8,128)S(1)}, u32[]{:S(2)}, u32[]{:S(2)}) %collective-permute-start.1) | collective-permute-done | bytes 458784 | tf_op jit(solution)/shard_map/ppermute | solution.py:396
  12.0 1.5 %collective-permute-done.above = f32[7,8,2048]{2,1,0:T(8,128)S(1)} collective-permute-done((f32[7,8,2048]{2,1,0:T(8,128)S(1)}, f32[7,8,2048]{2,1,0:T(8,128)S(1)}, u32[]{:S(2)}, u32[]{:S(2)}) %collective-permute-start) | collective-permute-done | bytes 458784 | tf_op jit(solution)/shard_map/ppermute | solution.py:395
  13.4 6.5 %down.1 = (f32[16,40,128]{2,1,0:T(8,128)S(1)}, f32[3,8,2048]{2,1,0:T(8,128)S(1)}, f32[48,1024]{1,0:T(8,128)S(1)}, f32[24,512]{1,0:T(8,128)S(1)}, f32[48,1024]{1,...) custom-call(s32[2]{0:T(128)S(1)} %pad_add_fusion.edge, ...), custom_call_target="tpu_custom_call" | custom-call | flops 20000000 | bytes 1048576 | tf_op jit(solution)/shard_map/down/pallas_call | solution.py:373
  20.0 33.9 %all_to_all.15 = f32[16,40,128]{2,1,0:T(8,128)S(1)} all-to-all(f32[16,40,128]{2,1,0:T(8,128)S(1)} %get-tuple-element.25), channel_id=1, replica_groups=mesh['level'=8,'slab_0'=4,'slab_1'=16] {'slab_1'}, dimensions={0} | all-to-all | bytes 655360 | tf_op jit(solution)/shard_map/all_to_all | solution.py:424
  53.9 0.9 broadcast_in_dim.10
  54.9 4.0 %all-to-all-start.1 = ((f32[4,16,24,128]{3,2,1,0:T(8,128)}), f32[4,16,24,128]{3,2,1,0:T(8,128)S(1)}, u32[]{:S(2)}, u32[]{:S(2)}) async-start(f32[4,16,24,128]{3,2,1,0:T(8,128)} %broadcast_in_dim.10), calls=%async_computation.1 | async-start | bytes 1572864 | tf_op jit(solution)/shard_map/all_to_all | solution.py:430
  58.9 8.3 %collective-permute-start.2 = (f32[8,512]{1,0:T(8,128)S(1)}, f32[8,512]{1,0:T(8,128)S(1)}, u32[]{:S(2)}, u32[]{:S(2)}) collective-permute-start(f32[8,512]{1,0:T(8,128)S(1)} %get-tuple-element.29), channel_id=1, source_target_pairs={{0,1},{1,2},{2,3},{3,4},{4,5},{5,6},{6,7},{7,8},{8,9},{9,10},{10,1... | collective-permute-start | bytes 49160 | tf_op jit(solution)/shard_map/ppermute | solution.py:426
  67.2 1.3 %collective-permute-start.3 = (f32[8,512]{1,0:T(8,128)S(1)}, f32[8,512]{1,0:T(8,128)S(1)}, u32[]{:S(2)}, u32[]{:S(2)}) collective-permute-start(f32[8,512]{1,0:T(8,128)S(1)} %get-tuple-element.30), channel_id=1, source_target_pairs={{1,0},{2,1},{3,2},{4,3},{5,4},{6,5},{7,6},{8,7},{9,8},{10,9},{11,1... | collective-permute-start | bytes 49160 | tf_op jit(solution)/shard_map/ppermute | solution.py:427
  68.5 0.1 pad_add_fusion.1.place
  69.2 0.0 collective-permute-done.2.top
  69.3 2.7 %collective-permute-done.3.bottom = f32[8,512]{1,0:T(8,128)S(1)} collective-permute-done((f32[8,512]{1,0:T(8,128)S(1)}, f32[8,512]{1,0:T(8,128)S(1)}, u32[]{:S(2)}, u32[]{:S(2)}) %collective-permute-start.3) | collective-permute-done | bytes 16416 | tf_op jit(solution)/shard_map/ppermute | solution.py:427
  72.0 0.0 all-to-all-done.1
  72.0 4.0 %coarse.1 = (f32[24,256]{1,0:T(8,128)S(1)}, f32[32,8,128]{2,1,0:T(8,128)}) custom-call(s32[3]{0:T(128)S(1)} %pad_add_fusion.1.place, s32[1]{0:T(128)S(6)} %copy.8.counts, f32[1536,128]{1,0:T(8,128)S(1)} %bitcast.8, f32[640,128]{1,0:T(8,128)S(1)} %bitcast.9, f32[8,512]{1,0:T(8,128)S(1)} %collective-permute-done.2.top, f32[8,512]{1,0:T(8,128)S(1)} %collective-permute-done.3.bottom), custom_call_target="tpu_custom_call" | custom-call | flops 5000000 | bytes 1048576 | tf_op jit(solution)/shard_map/coarse/pallas_call | solution.py:373
  76.0 0.0 copy-start
  76.0 0.0 copy-start.1
  76.0 12.5 %all-to-all-start.2 = ((f32[32,8,128]{2,1,0:T(8,128)}), f32[32,8,128]{2,1,0:T(8,128)S(1)}, u32[]{:S(2)}, u32[]{:S(2)}) async-start(f32[32,8,128]{2,1,0:T(8,128)} %get-tuple-element.32), calls=%async_computation.2 | async-start | bytes 262144 | tf_op jit(solution)/shard_map/all_to_all | solution.py:441
  88.5 0.0 copy-done
  88.5 0.0 copy-done.1
  88.6 2.6 %up.1 = f32[3,8,2048]{2,1,0:T(8,128)} custom-call(s32[2]{0:T(128)S(1)} %pad_add_fusion.edge, f32[3,8,2048]{2,1,0:T(8,128)S(1)} %copy-done, f32[8,2048]{1,0:T(8,128)S(1)} %copy-done.1, f32[3,8,2048]{2,1,0:T(8,128)S(1)} %get-tuple-element.20.rims, f32[48,1024]{1,0:T(8,128)S(1)} %get-tuple-element.21.s1, f32[24,512]{1,0:T(8,128)S(1)} %get-tuple-element.22.s2, ...), custom_call_target="tpu_custom_call" | custom-call | flops 10000000 | bytes 1048576 | tf_op jit(solution)/shard_map/up/pallas_call | solution.py:373
  91.2 5.0 %all-to-all-done.2.got = f32[32,8,128]{2,1,0:T(8,128)S(1)} async-done(((f32[32,8,128]{2,1,0:T(8,128)}), f32[32,8,128]{2,1,0:T(8,128)S(1)}, u32[]{:S(2)}, u32[]{:S(2)}) %all-to-all-start.2) | async-done | bytes 131104 | tf_op jit(solution)/shard_map/all_to_all | solution.py:441
  96.1 1.4 %final.1 = (f32[3]{0:T(128)}, f32[1,2]{1,0:T(1,128)}, f32[2]{0:T(128)}) custom-call(s32[3]{0:T(128)S(1)} %pad_add_fusion.1.place, f32[32,8,128]{2,1,0:T(8,128)S(1)} %all-to-all-done.2.got), custom_call_target="tpu_custom_call" | custom-call | flops 1000 | bytes 1048576 | tf_op jit(solution)/shard_map/final/pallas_call | solution.py:373
  (1 shorter events, 0.0 us)
Async XLA Ops:
  1.7 10.2 %collective-permute-start.1 = (f32[7,8,2048]{2,1,0:T(8,128)S(1)}, f32[7,8,2048]{2,1,0:T(8,128)S(1)}, u32[]{:S(2)}, u32[]{:S(2)}) collective-permute-start(f32[7,8,2048]{2,1,0:T(8,128)S(1)} %pad_maximum_fusion.here), channel_id=1, source_target_pairs={{1,0},{2,1},{3,2},{4,3},{5,4},{6,5},{7,6},{8,7},{9,8},{10,9},{11,1... | collective-permute-start | bytes 1376264 | tf_op jit(solution)/shard_map/ppermute | solution.py:396
  3.0 10.4 %collective-permute-start = (f32[7,8,2048]{2,1,0:T(8,128)S(1)}, f32[7,8,2048]{2,1,0:T(8,128)S(1)}, u32[]{:S(2)}, u32[]{:S(2)}) collective-permute-start(f32[7,8,2048]{2,1,0:T(8,128)S(1)} %pad_maximum_fusion.here), channel_id=1, source_target_pairs={{0,1},{1,2},{2,3},{3,4},{4,5},{5,6},{6,7},{7,8},{8,9},{9,10},{10,1... | collective-permute-start | bytes 1376264 | tf_op jit(solution)/shard_map/ppermute | solution.py:395
  54.9 17.1 %all-to-all-start.1 = ((f32[4,16,24,128]{3,2,1,0:T(8,128)}), f32[4,16,24,128]{3,2,1,0:T(8,128)S(1)}, u32[]{:S(2)}, u32[]{:S(2)}) async-start(f32[4,16,24,128]{3,2,1,0:T(8,128)} %broadcast_in_dim.10), calls=%async_computation.1 | async-start | bytes 1572864 | tf_op jit(solution)/shard_map/all_to_all | solution.py:430
  58.9 10.3 %collective-permute-start.2 = (f32[8,512]{1,0:T(8,128)S(1)}, f32[8,512]{1,0:T(8,128)S(1)}, u32[]{:S(2)}, u32[]{:S(2)}) collective-permute-start(f32[8,512]{1,0:T(8,128)S(1)} %get-tuple-element.29), channel_id=1, source_target_pairs={{0,1},{1,2},{2,3},{3,4},{4,5},{5,6},{6,7},{7,8},{8,9},{9,10},{10,1... | collective-permute-start | bytes 49160 | tf_op jit(solution)/shard_map/ppermute | solution.py:426
  67.2 4.8 %collective-permute-start.3 = (f32[8,512]{1,0:T(8,128)S(1)}, f32[8,512]{1,0:T(8,128)S(1)}, u32[]{:S(2)}, u32[]{:S(2)}) collective-permute-start(f32[8,512]{1,0:T(8,128)S(1)} %get-tuple-element.30), channel_id=1, source_target_pairs={{1,0},{2,1},{3,2},{4,3},{5,4},{6,5},{7,6},{8,7},{9,8},{10,9},{11,1... | collective-permute-start | bytes 49160 | tf_op jit(solution)/shard_map/ppermute | solution.py:427
  76.0 12.5 %copy-start = (f32[3,8,2048]{2,1,0:T(8,128)S(1)}, f32[3,8,2048]{2,1,0:T(8,128)}, u32[]{:S(2)}) copy-start(f32[3,8,2048]{2,1,0:T(8,128)} %here.1) | copy-start | bytes 589828
  76.0 12.5 %copy-start.1 = (f32[8,2048]{1,0:T(8,128)S(1)}, f32[8,2048]{1,0:T(8,128)}, u32[]{:S(2)}) copy-start(f32[8,2048]{1,0:T(8,128)} %g.1) | copy-start | bytes 196612
  76.0 20.1 %all-to-all-start.2 = ((f32[32,8,128]{2,1,0:T(8,128)}), f32[32,8,128]{2,1,0:T(8,128)S(1)}, u32[]{:S(2)}, u32[]{:S(2)}) async-start(f32[32,8,128]{2,1,0:T(8,128)} %get-tuple-element.32), calls=%async_computation.2 | async-start | bytes 262144 | tf_op jit(solution)/shard_map/all_to_all | solution.py:441

commit v2 on v1

--- a/solution.py
+++ b/solution.py
@@ -134,7 +134,7 @@
 
 
 def down_kernel(
-    edge, here, above, under,
+    edge, here, one, two,
     packed, rims, s1_out, s2_out, k1_out, k2_out, to_below, to_above,
     scratch, even, odd, parts,
 ):
@@ -143,13 +143,19 @@
     slots = fields // 2
     copies = packed.shape[0]
     chunks = here.shape[2] // 128
-    source = jnp.concatenate([above[fields], here[fields], under[fields]], axis=0)
+    flip = edge[2] == 1
+
+    def window(at):
+        a, b = one[at], two[at]
+        return jnp.concatenate([jnp.where(flip, b, a), here[at], jnp.where(flip, a, b)], axis=0)
+
+    source = window(fields)
     for q in range(3):
         for i in range(chunks):
             scratch[q, i * 32 + 24 : i * 32 + 32, :] = jnp.zeros((8, 128), F32)
 
     def finest(fine, field, _):
-        k = jnp.concatenate([above[field], here[field], under[field]], axis=0)
+        k = window(field)
         us, rs, rw, share = sweep(k, source, None, 0, 24, edge)
         parts[pl.ds(pl.multiple_of(field * 8, 8), 8), :] = summed(pieces(share[8:16]))
         if fine:
@@ -174,16 +180,16 @@
         span = slice(q * (chunks // 2) * block, (q + 1) * (chunks // 2) * block)
         got = dot(jnp.concatenate([even[span, :], odd[span, :]], axis=1), quarter)
         level.append(jnp.concatenate([got[i * block : (i + 1) * block] for i in range(chunks // 2)], axis=1))
-    for depth, window in ((1, 16), (2, 8)):
+    for depth, room in ((1, 16), (2, 8)):
         k, s, w = level
-        us, rs, rw, share = sweep(k, s, w, depth, window, edge)
+        us, rs, rw, share = sweep(k, s, w, depth, room, edge)
         own = 8 >> depth
-        row = iota(share.shape, 0) % window
+        row = iota(share.shape, 0) % room
         share = summed(pieces(jnp.where((row >= own) & (row < 2 * own), share, 0.0))) * (16.0**depth)
         for field in range(fields):
-            at = field * window
-            parts[field * 8 : field * 8 + 8, :] += summed([share[at + i : at + i + 8] for i in range(0, window, 8)])
-        kept = slots * window
+            at = field * room
+            parts[field * 8 : field * 8 + 8, :] += summed([share[at + i : at + i + 8] for i in range(0, room, 8)])
+        kept = slots * room
         if depth == 1:
             s1_out[...], k1_out[...] = s[:kept], k[:kept]
         else:
@@ -265,7 +271,6 @@
     for f in range(slots):
         total = total + jnp.where(lane == f, 64.0 * jnp.sum(weighed(f) - weighed(slots + f)), 0.0)
     sent = jnp.where(lane < slots, total / cells, jnp.where(lane == slots, counts[0].astype(F32), 0.0))
-    sent = jnp.broadcast_to(sent, (8, 128))
     for i in range(message.shape[0]):
         message[i] = sent
 
@@ -369,7 +374,7 @@
     return jax.ShapeDtypeStruct(dims, F32)
 
 
-def call(kernel, outs, smem, vmem, scratch, flops, name, mib, scalars=0):
+def call(kernel, outs, smem, vmem, scratch, flops, mib, scalars=0):
     return pl.pallas_call(
         kernel,
         out_shape=outs,
@@ -378,7 +383,6 @@
         scratch_shapes=[pltpu.VMEM(s, F32) for s in scratch],
         compiler_params=pltpu.CompilerParams(vmem_limit_bytes=mib << 20),
         cost_estimate=pl.CostEstimate(flops=flops, bytes_accessed=1 << 20, transcendentals=0),
-        name=name,
     )(*smem, *vmem)
 
 
@@ -392,9 +396,11 @@
     from_above = [(i, i + 1) for i in range(slabs - 1)]
     from_below = [(i + 1, i) for i in range(slabs - 1)]
     here = jnp.concatenate([coef_fine, coef_coarse, rhs_field[None]], axis=0)
-    above = lax.ppermute(here, SLAB, from_above)
-    under = lax.ppermute(here, SLAB, from_below)
-    edge = jnp.stack([jnp.where(me == 0, 8, 0), jnp.where(me == slabs - 1, 16, 24)]).astype(jnp.int32)
+    odd_down = [pair for i in range(1, slabs - 1, 2) for pair in ((i, i + 1), (i + 1, i))]
+    odd_up = [pair for i in range(0, slabs, 2) for pair in ((i, i + 1), (i + 1, i))]
+    one = lax.ppermute(here, SLAB, odd_down)
+    two = lax.ppermute(here, SLAB, odd_up)
+    edge = jnp.stack([jnp.where(me == 0, 8, 0), jnp.where(me == slabs - 1, 16, 24), me % 2]).astype(jnp.int32)
     place = jnp.stack([me, lax.axis_index("slab_0"), lax.axis_index("level")]).astype(jnp.int32)
 
     packed, rims, s1, s2, k1, k2, to_below, to_above = call(
@@ -410,7 +416,7 @@
             shape(8, cols // 4),
         ],
         [edge],
-        [here, above, under],
+        [here, one, two],
         [
             (3, max(cols // 4, 768), 128),
             (3 * fields * cols // 16, 128),
@@ -418,7 +424,6 @@
             (fields * 8, 128),
         ],
         20_000_000,
-        "down",
         28,
     )
     lines = lax.all_to_all(packed, "slab_1", 0, 0, tiled=True)
@@ -430,12 +435,11 @@
     gathered = lax.all_to_all(wide, "slab_0", 0, 0, tiled=True).reshape(slabs * used, 128)
     e3, message = call(
         functools.partial(coarse_kernel, fields=fields, slabs=slabs, rows=inner, cells=float(rows * slabs * cols)),
-        [shape(slots * 8, 256), shape(levels * outer, 8, 128)],
+        [shape(slots * 8, 256), shape(levels * outer, 1, 128)],
         [place, level_counts],
         [gathered, lines.reshape(inner * LINES, 128), top, bottom],
         [(2, 2 * fields * slabs, 128), (fields * slabs + 16, 256)],
         5_000_000,
-        "coarse",
         16,
     )
     got = lax.all_to_all(message, ("level", "slab_0"), 0, 0, tiled=True)
@@ -446,7 +450,6 @@
         [coef_fine, rhs_field, rims, s1, s2, k1, k2, e3, top, bottom],
         [(cols // 2, 128)],
         10_000_000,
-        "up",
         16,
     )
     diffs, moments, estimate = call(
@@ -456,7 +459,6 @@
         [got],
         [],
         1_000,
-        "final",
         4,
         3,
     )

time: 97.9 us -> 97.7 us (level)
  blocking collectives: 33.9 us -> 36 us
  starting transfers between devices: 32.4 us -> 30.8 us
    all_to_all x1, blocking collectives: 33.9 us -> 36 us  [on_device(): lines = lax.all_to_all(packed, 'slab_1', 0, 0, tiled=True)]
    ppermute x2, starting transfers between devices: 6.31 us -> 5.05 us  [the longest x1 4.36 us: on_device(): two = lax.ppermute(here, SLAB, odd_up)]
  transfers between devices with their start and end apart: 6 -> 6, of which waited for: 4 -> 3; matrix products, arithmetic and copies ran while one was open for 0% -> 0% of each run, Pallas kernels for 3% -> 3%
where the time goes in v2:
time: 97.7 us; the launch traced here: 97.4 us
  blocking collectives  36 us (37%)
  starting transfers between devices  30.8 us (32%)
  Pallas kernels  14.7 us (15%)
  waiting for transfers between devices  12.1 us (12%)
  between operations  1.39 us (1%)
  other arithmetic  1.24 us (1%)
    all_to_all x1, blocking collectives, on_device(): lines = lax.all_to_all(packed, 'slab_1', 0, 0, tiled=True)  36 us
    pallas_call x4, Pallas kernels, call(): pl.pallas_call(kernel, out_shape=outs, in_specs=[SMEM] * len(smem) + [VME...  14.7 us
    all_to_all x1, starting transfers between devices, on_device(): got = lax.all_to_all(message, ('level', 'slab_0'), 0, 0, tiled=True)  11.5 us
    ppermute x1, starting transfers between devices, on_device(): top = lax.ppermute(to_below, SLAB, from_above)  8.95 us
    ppermute x1, waiting for transfers between devices, on_device(): two = lax.ppermute(here, SLAB, odd_up)  5.06 us
    ppermute x1, starting transfers between devices, on_device(): two = lax.ppermute(here, SLAB, odd_up)  4.36 us
    all_to_all x1, waiting for transfers between devices, on_device(): got = lax.all_to_all(message, ('level', 'slab_0'), 0, 0, tiled=True)  4.34 us
    all_to_all x1, starting transfers between devices, on_device(): lax.all_to_all(wide, 'slab_0', 0, 0, tiled=True).reshape(slabs * used, 128)  4.01 us
  transfers between devices with their start and end apart: 6, of which 3 were waited for; matrix products, arithmetic and copies ran while one was open for 0% of the time, Pallas kernels for 3%

profile of v2, /device:TPU:1, one launch (start us, length us, event | category | flops | bytes accessed | tf_op | source)
XLA Modules:
  0.0 97.4 jit_solution(976450596866227466)
XLA Ops:
  0.6 1.1 %pad_maximum_fusion.here = f32[7,8,2048]{2,1,0:T(8,128)S(1)} fusion(f32[1,8,2048]{2,1,0:T(8,128)} %bitcast.11, f32[3,8,2048]{2,1,0:T(8,128)} %param.5, f32[3,8,2048]{2,1,0:T(8,128)} %here.1), kind=kLoop, calls=%fused_computation | loop fusion | flops 229376 | bytes 917504 | tf_op jit(solution)/shard_map/concatenate | solution.py:398
  1.7 4.4 %collective-permute-start.1 = (f32[7,8,2048]{2,1,0:T(8,128)S(1)}, f32[7,8,2048]{2,1,0:T(8,128)S(1)}, u32[]{:S(2)}, u32[]{:S(2)}) collective-permute-start(f32[7,8,2048]{2,1,0:T(8,128)S(1)} %pad_maximum_fusion.here), channel_id=1, source_target_pairs={{0,1},{1,0},{2,3},{3,2},{4,5},{5,4},{6,7},{7,6},{8,9},{9,8},{10,11... | collective-permute-start | bytes 1376264 | tf_op jit(solution)/shard_map/ppermute | solution.py:402
  6.1 0.7 collective-permute-start
  6.8 0.1 pad_add_fusion.edge
  6.9 5.1 %collective-permute-done.1.two = f32[7,8,2048]{2,1,0:T(8,128)S(1)} collective-permute-done((f32[7,8,2048]{2,1,0:T(8,128)S(1)}, f32[7,8,2048]{2,1,0:T(8,128)S(1)}, u32[]{:S(2)}, u32[]{:S(2)}) %collective-permute-start.1) | collective-permute-done | bytes 458784 | tf_op jit(solution)/shard_map/ppermute | solution.py:402
  12.0 0.0 collective-permute-done.one
  12.0 6.8 %shard_map.75 = (f32[16,40,128]{2,1,0:T(8,128)S(1)}, f32[3,8,2048]{2,1,0:T(8,128)S(1)}, f32[48,1024]{1,0:T(8,128)S(1)}, f32[24,512]{1,0:T(8,128)S(1)}, f32[48,10...) custom-call(s32[3]{0:T(128)S(1)} %pad_add_fusion.edge, ...), custom_call_target="tpu_custom_call" | custom-call | flops 20000000 | bytes 1048576 | tf_op jit(solution)/shard_map/pallas_call | solution.py:378
  18.7 36.0 %all_to_all.15 = f32[16,40,128]{2,1,0:T(8,128)S(1)} all-to-all(f32[16,40,128]{2,1,0:T(8,128)S(1)} %get-tuple-element.25), channel_id=1, replica_groups=mesh['level'=8,'slab_0'=4,'slab_1'=16] {'slab_1'}, dimensions={0} | all-to-all | bytes 655360 | tf_op jit(solution)/shard_map/all_to_all | solution.py:429
  54.8 0.9 broadcast_in_dim.10
  55.7 4.0 %all-to-all-start.1 = ((f32[4,16,24,128]{3,2,1,0:T(8,128)}), f32[4,16,24,128]{3,2,1,0:T(8,128)S(1)}, u32[]{:S(2)}, u32[]{:S(2)}) async-start(f32[4,16,24,128]{3,2,1,0:T(8,128)} %broadcast_in_dim.10), calls=%async_computation.1 | async-start | bytes 1572864 | tf_op jit(solution)/shard_map/all_to_all | solution.py:435
  59.7 9.0 %collective-permute-start.2 = (f32[8,512]{1,0:T(8,128)S(1)}, f32[8,512]{1,0:T(8,128)S(1)}, u32[]{:S(2)}, u32[]{:S(2)}) collective-permute-start(f32[8,512]{1,0:T(8,128)S(1)} %get-tuple-element.29), channel_id=1, source_target_pairs={{0,1},{1,2},{2,3},{3,4},{4,5},{5,6},{6,7},{7,8},{8,9},{9,10},{10,1... | collective-permute-start | bytes 49160 | tf_op jit(solution)/shard_map/ppermute | solution.py:431
  68.7 1.3 %collective-permute-start.3 = (f32[8,512]{1,0:T(8,128)S(1)}, f32[8,512]{1,0:T(8,128)S(1)}, u32[]{:S(2)}, u32[]{:S(2)}) collective-permute-start(f32[8,512]{1,0:T(8,128)S(1)} %get-tuple-element.30), channel_id=1, source_target_pairs={{1,0},{2,1},{3,2},{4,3},{5,4},{6,5},{7,6},{8,7},{9,8},{10,9},{11,1... | collective-permute-start | bytes 49160 | tf_op jit(solution)/shard_map/ppermute | solution.py:432
  70.0 0.1 pad_add_fusion.1.place
  70.7 0.0 collective-permute-done.2.top
  70.7 2.7 %collective-permute-done.3.bottom = f32[8,512]{1,0:T(8,128)S(1)} collective-permute-done((f32[8,512]{1,0:T(8,128)S(1)}, f32[8,512]{1,0:T(8,128)S(1)}, u32[]{:S(2)}, u32[]{:S(2)}) %collective-permute-start.3) | collective-permute-done | bytes 16416 | tf_op jit(solution)/shard_map/ppermute | solution.py:432
  73.5 0.0 all-to-all-done.1
  73.5 0.0 copy-start
  73.5 0.0 copy-start.1
  73.5 4.0 %shard_map.76 = (f32[24,256]{1,0:T(8,128)S(1)}, f32[32,1,128]{2,1,0:T(1,128)}) custom-call(s32[3]{0:T(128)S(1)} %pad_add_fusion.1.place, s32[1]{0:T(128)S(6)} %copy.8.counts, f32[1536,128]{1,0:T(8,128)S(1)} %bitcast.9, f32[640,128]{1,0:T(8,128)S(1)} %bitcast.10, f32[8,512]{1,0:T(8,128)S(1)} %collective-permute-done.2.top, ...), custom_call_target="tpu_custom_call" | custom-call | flops 5000000 | bytes 1048576 | tf_op jit(solution)/shard_map/pallas_call | solution.py:378
  77.4 11.5 %all-to-all-start.2 = ((f32[32,1,128]{2,1,0:T(1,128)}), f32[32,1,128]{2,1,0:T(1,128)S(1)}, u32[]{:S(2)}, u32[]{:S(2)}) async-start(f32[32,1,128]{2,1,0:T(1,128)} %get-tuple-element.32), calls=%async_computation.2 | async-start | bytes 32768 | tf_op jit(solution)/shard_map/all_to_all | solution.py:445
  89.0 0.0 copy-done
  89.0 0.0 copy-done.1
  89.0 2.6 %shard_map.77 = f32[3,8,2048]{2,1,0:T(8,128)} custom-call(s32[3]{0:T(128)S(1)} %pad_add_fusion.edge, f32[3,8,2048]{2,1,0:T(8,128)S(1)} %copy-done, f32[8,2048]{1,0:T(8,128)S(1)} %copy-done.1, f32[3,8,2048]{2,1,0:T(8,128)S(1)} %get-tuple-element.20.rims, f32[48,1024]{1,0:T(8,128)S(1)} %get-tuple-element.21.s1, f32[24,512]{1,0:T(8,128)S(1)} %get-tuple-element.22.s2, ...), custom_call_target="tpu_custom_call" | custom-call | flops 10000000 | bytes 1048576 | tf_op jit(solution)/shard_map/pallas_call | solution.py:378
  91.6 4.3 %all-to-all-done.2.got = f32[32,1,128]{2,1,0:T(1,128)S(1)} async-done(((f32[32,1,128]{2,1,0:T(1,128)}), f32[32,1,128]{2,1,0:T(1,128)S(1)}, u32[]{:S(2)}, u32[]{:S(2)}) %all-to-all-start.2) | async-done | bytes 16416 | tf_op jit(solution)/shard_map/all_to_all | solution.py:445
  95.9 1.4 %shard_map.78 = (f32[3]{0:T(128)}, f32[1,2]{1,0:T(1,128)}, f32[2]{0:T(128)}) custom-call(s32[3]{0:T(128)S(1)} %pad_add_fusion.1.place, f32[32,1,128]{2,1,0:T(1,128)S(1)} %all-to-all-done.2.got), custom_call_target="tpu_custom_call" | custom-call | flops 1000 | bytes 1048576 | tf_op jit(solution)/shard_map/pallas_call | solution.py:378
  (1 shorter events, 0.0 us)
Async XLA Ops:
  1.7 10.2 %collective-permute-start.1 = (f32[7,8,2048]{2,1,0:T(8,128)S(1)}, f32[7,8,2048]{2,1,0:T(8,128)S(1)}, u32[]{:S(2)}, u32[]{:S(2)}) collective-permute-start(f32[7,8,2048]{2,1,0:T(8,128)S(1)} %pad_maximum_fusion.here), channel_id=1, source_target_pairs={{0,1},{1,0},{2,3},{3,2},{4,5},{5,4},{6,7},{7,6},{8,9},{9,8},{10,11... | collective-permute-start | bytes 1376264 | tf_op jit(solution)/shard_map/ppermute | solution.py:402
  6.1 5.9 %collective-permute-start = (f32[7,8,2048]{2,1,0:T(8,128)S(1)}, f32[7,8,2048]{2,1,0:T(8,128)S(1)}, u32[]{:S(2)}, u32[]{:S(2)}) collective-permute-start(f32[7,8,2048]{2,1,0:T(8,128)S(1)} %pad_maximum_fusion.here), channel_id=1, source_target_pairs={{1,2},{2,1},{3,4},{4,3},{5,6},{6,5},{7,8},{8,7},{9,10},{10,9},{11,... | collective-permute-start | bytes 1376264 | tf_op jit(solution)/shard_map/ppermute | solution.py:401
  55.7 17.8 %all-to-all-start.1 = ((f32[4,16,24,128]{3,2,1,0:T(8,128)}), f32[4,16,24,128]{3,2,1,0:T(8,128)S(1)}, u32[]{:S(2)}, u32[]{:S(2)}) async-start(f32[4,16,24,128]{3,2,1,0:T(8,128)} %broadcast_in_dim.10), calls=%async_computation.1 | async-start | bytes 1572864 | tf_op jit(solution)/shard_map/all_to_all | solution.py:435
  59.7 11.0 %collective-permute-start.2 = (f32[8,512]{1,0:T(8,128)S(1)}, f32[8,512]{1,0:T(8,128)S(1)}, u32[]{:S(2)}, u32[]{:S(2)}) collective-permute-start(f32[8,512]{1,0:T(8,128)S(1)} %get-tuple-element.29), channel_id=1, source_target_pairs={{0,1},{1,2},{2,3},{3,4},{4,5},{5,6},{6,7},{7,8},{8,9},{9,10},{10,1... | collective-permute-start | bytes 49160 | tf_op jit(solution)/shard_map/ppermute | solution.py:431
  68.7 4.8 %collective-permute-start.3 = (f32[8,512]{1,0:T(8,128)S(1)}, f32[8,512]{1,0:T(8,128)S(1)}, u32[]{:S(2)}, u32[]{:S(2)}) collective-permute-start(f32[8,512]{1,0:T(8,128)S(1)} %get-tuple-element.30), channel_id=1, source_target_pairs={{1,0},{2,1},{3,2},{4,3},{5,4},{6,5},{7,6},{8,7},{9,8},{10,9},{11,1... | collective-permute-start | bytes 49160 | tf_op jit(solution)/shard_map/ppermute | solution.py:432
  73.5 15.5 %copy-start = (f32[3,8,2048]{2,1,0:T(8,128)S(1)}, f32[3,8,2048]{2,1,0:T(8,128)}, u32[]{:S(2)}) copy-start(f32[3,8,2048]{2,1,0:T(8,128)} %here.1) | copy-start | bytes 589828
  73.5 15.5 %copy-start.1 = (f32[8,2048]{1,0:T(8,128)S(1)}, f32[8,2048]{1,0:T(8,128)}, u32[]{:S(2)}) copy-start(f32[8,2048]{1,0:T(8,128)} %g.1) | copy-start | bytes 196612
  77.4 18.5 %all-to-all-start.2 = ((f32[32,1,128]{2,1,0:T(1,128)}), f32[32,1,128]{2,1,0:T(1,128)S(1)}, u32[]{:S(2)}, u32[]{:S(2)}) async-start(f32[32,1,128]{2,1,0:T(1,128)} %get-tuple-element.32), calls=%async_computation.2 | async-start | bytes 32768 | tf_op jit(solution)/shard_map/all_to_all | solution.py:445

commit v3 on v2

--- a/solution.py
+++ b/solution.py
@@ -20,7 +20,15 @@
 
 def right_of(x, cols):
     n = x.shape[1]
-    return jnp.where(iota(x.shape, 1) == cols - 1, 0.0, pltpu.roll(x, n - 1, 1))
+    y = pltpu.roll(x, n - 1, 1)
+    edge = cols - 1 - (n - 128)
+    last = jnp.where(iota((x.shape[0], 128), 1) == edge, 0.0, y[:, n - 128 :])
+    return last if n == 128 else jnp.concatenate([y[:, : n - 128], last], axis=1)
+
+
+def first_column(x, edge):
+    first = jnp.where(iota((x.shape[0], 128), 1) == 0, edge[:, :128], x[:, :128])
+    return first if x.shape[1] == 128 else jnp.concatenate([first, x[:, 128:]], axis=1)
 
 
 def below(x, period):
@@ -33,9 +41,8 @@
 
 def faces(k, cols, period):
     half = 0.5 * k
-    first = iota(k.shape, 1) == 0
     fr = half + right_of(half, cols)
-    fl = jnp.where(first, half, pltpu.roll(fr, 1, 1))
+    fl = first_column(pltpu.roll(fr, 1, 1), half)
     fd = half + below(half, period)
     fu = pltpu.roll(fd, 1, 0)
     if period is not None:
@@ -45,7 +52,7 @@
 
 def across(u, half, fr, cols):
     q = fr * (u - right_of(u, cols))
-    return q - jnp.where(iota(u.shape, 1) == 0, -half * u, pltpu.roll(q, 1, 1))
+    return q - first_column(pltpu.roll(q, 1, 1), -half[:, :128] * u[:, :128])
 
 
 def fluxes(u, half, fr, fd, cols, period):
@@ -216,24 +223,43 @@
         packed[i] = packed[0]
 
 
-def coarse_kernel(place, counts, gathered, lines, top, bottom, e3, message, scratch, whole, *, fields, slabs, rows, cells):
-    del top, bottom
+def shared_lines(fields):
+    slots = fields // 2
+    common = [(q * fields + f) * 2 + h for q in range(2) for f in range(slots) for h in range(2)]
+    return common, lambda x: [(q * fields + slots + min(x, slots - 1)) * 2 + h for q in range(3) for h in range(2)]
+
+
+def fan_kernel(lines, wide, *, fields):
+    outer = wide.shape[0]
+    common, special = shared_lines(fields)
+    rows = wide.shape[1] // (len(common) + 6)
+    for at, line in enumerate(common):
+        got = lines[pl.ds(line, rows, stride=LINES), :]
+        for x in range(outer):
+            wide[x, at * rows : (at + 1) * rows, :] = got
+    for x in range(outer):
+        for at, line in enumerate(special(x)):
+            start = (len(common) + at) * rows
+            wide[x, start : start + rows, :] = lines[pl.ds(line, rows, stride=LINES), :]
+
+
+def coarse_kernel(place, counts, gathered, lines, e3, message, scratch, whole, *, fields, slabs, rows, cells):
     slots = fields // 2
     quarter = pair_matrix((256, 128), 0, 0.25)
     spread = pair_matrix((128, 256), 1, 1.0)
-    stride = 4 * fields
     n = slabs
-
-    def taken(q):
-        halves = [
-            jnp.concatenate(
-                [gathered[pl.ds((q * fields + f) * 2 + h, n, stride=stride), :] for f in range(fields)], axis=0
-            )
-            for h in range(2)
-        ]
-        return jnp.concatenate(halves, axis=1)
-
-    k3, s3 = taken(0), taken(1)
+    outer = gathered.shape[0]
+    common = 4 * slots
+
+    def taken(at):
+        return jnp.concatenate([gathered[x, at * rows : (at + 1) * rows, :] for x in range(outer)], axis=0)
+
+    def field(q, f):
+        if f == slots:
+            return jnp.concatenate([taken(common + q * 2), taken(common + q * 2 + 1)], axis=1)
+        return jnp.concatenate([taken((q * slots + f) * 2), taken((q * slots + f) * 2 + 1)], axis=1)
+
+    k3, s3 = [jnp.concatenate([field(q, f) for f in range(slots + 1)], axis=0) for q in range(2)]
     half3, fr3, fd3, diag3 = faces(k3, 256, n)
     scale3 = OMEGA / diag3
     u3 = scale3 * s3
@@ -255,8 +281,8 @@
     u3 = u3 + scale3 * (s3 - fluxes(u3, half3, fr3, fd3, 256, n))
     v3 = u3 * 64.0
     whole[0:8, :] = jnp.zeros((8, 256), F32)
-    whole[8 : 8 + fields * n, :] = v3
-    whole[8 + fields * n :, :] = jnp.zeros((8, 256), F32)
+    whole[8 : 8 + slots * n, :] = v3[: slots * n]
+    whole[8 + slots * n :, :] = jnp.zeros((8, 256), F32)
 
     lane = iota((1, 128), 1)
     block = pl.multiple_of(place[1] * rows, 8)
@@ -269,7 +295,9 @@
     total = jnp.sum(lines[pl.ds(6 * fields, rows, stride=LINES), :], axis=0, keepdims=True)
     total = total - pltpu.roll(total, 128 - slots, 1)
     for f in range(slots):
-        total = total + jnp.where(lane == f, 64.0 * jnp.sum(weighed(f) - weighed(slots + f)), 0.0)
+        total = total + jnp.where(lane == f, 64.0 * jnp.sum(weighed(f)), 0.0)
+    other = field(2, slots) * v3[slots * n :]
+    total = total - jnp.where((lane == place[1]) & (lane < slots), 64.0 * jnp.sum(other), 0.0)
     sent = jnp.where(lane < slots, total / cells, jnp.where(lane == slots, counts[0].astype(F32), 0.0))
     for i in range(message.shape[0]):
         message[i] = sent
@@ -325,7 +353,7 @@
         k = here[f]
         half = 0.5 * k
         fr = half + right_of(half, cols)
-        fl = jnp.where(iota(k.shape, 1) == 0, half, pltpu.roll(fr, 1, 1))
+        fl = first_column(pltpu.roll(fr, 1, 1), half)
         fd = half + lower(half, 0.5 * rims[f, 1:2, :])
         fu = half + upper(half, 0.5 * rims[f, 0:1, :])
         scale = OMEGA / ((fr + fl) + (fd + fu))
@@ -427,18 +455,26 @@
         28,
     )
     lines = lax.all_to_all(packed, "slab_1", 0, 0, tiled=True)
-    lines, to_below, to_above = lax.optimization_barrier((lines, to_below, to_above))
     top = lax.ppermute(to_below, SLAB, from_above)
     bottom = lax.ppermute(to_above, SLAB, from_below)
-    used = 4 * fields
-    wide = jnp.broadcast_to(lines[None, :, :used], (outer, inner, used, 128))
-    gathered = lax.all_to_all(wide, "slab_0", 0, 0, tiled=True).reshape(slabs * used, 128)
+    lines, top, bottom = lax.optimization_barrier((lines, top, bottom))
+    lines = lines.reshape(inner * LINES, 128)
+    (wide,) = call(
+        functools.partial(fan_kernel, fields=fields),
+        [shape(outer, (4 * slots + 6) * inner, 128)],
+        [],
+        [lines],
+        [],
+        1_000_000,
+        8,
+    )
+    gathered = lax.all_to_all(wide, "slab_0", 0, 0, tiled=True)
     e3, message = call(
         functools.partial(coarse_kernel, fields=fields, slabs=slabs, rows=inner, cells=float(rows * slabs * cols)),
         [shape(slots * 8, 256), shape(levels * outer, 1, 128)],
         [place, level_counts],
-        [gathered, lines.reshape(inner * LINES, 128), top, bottom],
-        [(2, 2 * fields * slabs, 128), (fields * slabs + 16, 256)],
+        [gathered, lines],
+        [(2, 2 * (slots + 1) * slabs, 128), (slots * slabs + 16, 256)],
         5_000_000,
         16,
     )

time: 97.7 us -> 94.9 us (0.971)
  blocking collectives: 36 us -> 0 us
  starting transfers between devices: 30.8 us -> 50.8 us
  waiting for transfers between devices: 12.1 us -> 25.2 us
  Pallas kernels: 14.7 us -> 15.9 us
    all_to_all x1 -> x0, blocking collectives: 36 us -> none  [on_device(): lines = lax.all_to_all(packed, 'slab_1', 0, 0, tiled=True)]
    all_to_all x1 -> x2, starting transfers between devices: 4.01 us -> 26.4 us  [the longest x1 22.4 us: on_device(): lines = lax.all_to_all(packed, 'slab_1', 0, 0, tiled=True)]
    all_to_all x1 -> x2, waiting for transfers between devices: 0.01 us -> 7.42 us  [the longest x1 6.55 us: on_device(): gathered = lax.all_to_all(wide, 'slab_0', 0, 0, tiled=True)]
    ppermute x1, starting transfers between devices: 8.95 us -> 3.26 us  [on_device(): top = lax.ppermute(to_below, SLAB, from_above)]
    ppermute x1, waiting for transfers between devices: 2.74 us -> 7.15 us  [on_device(): bottom = lax.ppermute(to_above, SLAB, from_below)]
    all_to_all x1, starting transfers between devices: 11.5 us -> 14.8 us  [on_device(): got = lax.all_to_all(message, ('level', 'slab_0'), 0, 0, tiled=True)]
    ppermute x1, waiting for transfers between devices: 0.01 us -> 1.25 us  [on_device(): top = lax.ppermute(to_below, SLAB, from_above)]
    pallas_call x4 -> x5, Pallas kernels: 14.7 us -> 15.9 us  [call(): pl.pallas_call(kernel, out_shape=outs, in_specs=[SMEM] * len(smem) + [VME...]
  transfers between devices with their start and end apart: 6 -> 7, of which waited for: 3 -> 6; matrix products, arithmetic and copies ran while one was open for 0% -> 0% of each run, Pallas kernels for 3% -> 3%
where the time goes in v3:
time: 94.9 us; the launch traced here: 94.5 us
  starting transfers between devices  50.8 us (54%)
  waiting for transfers between devices  25.2 us (27%)
  Pallas kernels  15.9 us (17%)
  between operations  1.38 us (1%)
  other arithmetic  1.24 us (1%)
    all_to_all x1, starting transfers between devices, on_device(): lines = lax.all_to_all(packed, 'slab_1', 0, 0, tiled=True)  22.4 us
    pallas_call x5, Pallas kernels, call(): pl.pallas_call(kernel, out_shape=outs, in_specs=[SMEM] * len(smem) + [VME...  15.9 us
    all_to_all x1, starting transfers between devices, on_device(): got = lax.all_to_all(message, ('level', 'slab_0'), 0, 0, tiled=True)  14.8 us
    ppermute x1, waiting for transfers between devices, on_device(): bottom = lax.ppermute(to_above, SLAB, from_below)  7.15 us
    all_to_all x1, waiting for transfers between devices, on_device(): gathered = lax.all_to_all(wide, 'slab_0', 0, 0, tiled=True)  6.55 us
    ppermute x1, waiting for transfers between devices, on_device(): two = lax.ppermute(here, SLAB, odd_up)  5.06 us
    ppermute x1, starting transfers between devices, on_device(): two = lax.ppermute(here, SLAB, odd_up)  4.36 us
    all_to_all x1, waiting for transfers between devices, on_device(): got = lax.all_to_all(message, ('level', 'slab_0'), 0, 0, tiled=True)  4.33 us
  transfers between devices with their start and end apart: 7, of which 6 were waited for; matrix products, arithmetic and copies ran while one was open for 0% of the time, Pallas kernels for 3%

profile of v3, /device:TPU:1, one launch (start us, length us, event | category | flops | bytes accessed | tf_op | source)
XLA Modules:
  0.0 94.5 jit_solution(6082955702177547709)
XLA Ops:
  0.6 1.1 %pad_maximum_fusion.here = f32[7,8,2048]{2,1,0:T(8,128)S(1)} fusion(f32[1,8,2048]{2,1,0:T(8,128)} %bitcast.10, f32[3,8,2048]{2,1,0:T(8,128)} %param.5, f32[3,8,2048]{2,1,0:T(8,128)} %here.1), kind=kLoop, calls=%fused_computation | loop fusion | flops 229376 | bytes 917504 | tf_op jit(solution)/shard_map/concatenate | solution.py:426
  1.7 4.4 %collective-permute-start.1 = (f32[7,8,2048]{2,1,0:T(8,128)S(1)}, f32[7,8,2048]{2,1,0:T(8,128)S(1)}, u32[]{:S(2)}, u32[]{:S(2)}) collective-permute-start(f32[7,8,2048]{2,1,0:T(8,128)S(1)} %pad_maximum_fusion.here), channel_id=1, source_target_pairs={{0,1},{1,0},{2,3},{3,2},{4,5},{5,4},{6,7},{7,6},{8,9},{9,8},{10,11... | collective-permute-start | bytes 1376264 | tf_op jit(solution)/shard_map/ppermute | solution.py:430
  6.1 0.7 collective-permute-start
  6.8 0.1 pad_add_fusion.edge
  6.9 5.1 %collective-permute-done.1.two = f32[7,8,2048]{2,1,0:T(8,128)S(1)} collective-permute-done((f32[7,8,2048]{2,1,0:T(8,128)S(1)}, f32[7,8,2048]{2,1,0:T(8,128)S(1)}, u32[]{:S(2)}, u32[]{:S(2)}) %collective-permute-start.1) | collective-permute-done | bytes 458784 | tf_op jit(solution)/shard_map/ppermute | solution.py:430
  12.0 0.0 collective-permute-done.one
  12.0 7.5 %shard_map.75 = (f32[16,40,128]{2,1,0:T(8,128)}, f32[3,8,2048]{2,1,0:T(8,128)S(1)}, f32[48,1024]{1,0:T(8,128)S(1)}, f32[24,512]{1,0:T(8,128)S(1)}, f32[48,1024]{...) custom-call(s32[3]{0:T(128)S(1)} %pad_add_fusion.edge, ...), custom_call_target="tpu_custom_call" | custom-call | flops 20000000 | bytes 1048576 | tf_op jit(solution)/shard_map/pallas_call | solution.py:406
  19.4 22.4 %all-to-all-start = ((f32[16,40,128]{2,1,0:T(8,128)}), f32[16,40,128]{2,1,0:T(8,128)S(1)}, u32[]{:S(2)}, u32[]{:S(2)}) async-start(f32[16,40,128]{2,1,0:T(8,128)} %get-tuple-element.25), calls=%async_computation | async-start | bytes 655360 | tf_op jit(solution)/shard_map/all_to_all | solution.py:457
  41.8 3.3 %collective-permute-start.2 = (f32[8,512]{1,0:T(8,128)S(1)}, f32[8,512]{1,0:T(8,128)S(1)}, u32[]{:S(2)}, u32[]{:S(2)}) collective-permute-start(f32[8,512]{1,0:T(8,128)S(1)} %get-tuple-element.26), channel_id=1, source_target_pairs={{0,1},{1,2},{2,3},{3,4},{4,5},{5,6},{6,7},{7,8},{8,9},{9,10},{10,1... | collective-permute-start | bytes 49160 | tf_op jit(solution)/shard_map/ppermute | solution.py:458
  45.1 1.3 %collective-permute-start.3 = (f32[8,512]{1,0:T(8,128)S(1)}, f32[8,512]{1,0:T(8,128)S(1)}, u32[]{:S(2)}, u32[]{:S(2)}) collective-permute-start(f32[8,512]{1,0:T(8,128)S(1)} %get-tuple-element.27), channel_id=1, source_target_pairs={{1,0},{2,1},{3,2},{4,3},{5,4},{6,5},{7,6},{8,7},{9,8},{10,9},{11,1... | collective-permute-start | bytes 49160 | tf_op jit(solution)/shard_map/ppermute | solution.py:459
  46.4 1.2 %collective-permute-done.2.top = f32[8,512]{1,0:T(8,128)S(1)} collective-permute-done((f32[8,512]{1,0:T(8,128)S(1)}, f32[8,512]{1,0:T(8,128)S(1)}, u32[]{:S(2)}, u32[]{:S(2)}) %collective-permute-start.2) | collective-permute-done | bytes 16416 | tf_op jit(solution)/shard_map/ppermute | solution.py:458
  47.6 7.2 %collective-permute-done.3.bottom = f32[8,512]{1,0:T(8,128)S(1)} collective-permute-done((f32[8,512]{1,0:T(8,128)S(1)}, f32[8,512]{1,0:T(8,128)S(1)}, u32[]{:S(2)}, u32[]{:S(2)}) %collective-permute-start.3) | collective-permute-done | bytes 16416 | tf_op jit(solution)/shard_map/ppermute | solution.py:459
  54.8 0.9 all-to-all-done
  55.7 0.9 shard_map.76
  56.5 4.0 %all-to-all-start.1 = ((f32[4,288,128]{2,1,0:T(8,128)}), f32[4,288,128]{2,1,0:T(8,128)S(1)}, u32[]{:S(2)}, u32[]{:S(2)}) async-start(f32[4,288,128]{2,1,0:T(8,128)} %shard_map.76), calls=%async_computation.1 | async-start | bytes 1179648 | tf_op jit(solution)/shard_map/all_to_all | solution.py:471
  61.2 0.1 pad_add_fusion.1.place
  61.3 0.0 copy-start
  61.3 6.6 %all-to-all-done.1.gathered = f32[4,288,128]{2,1,0:T(8,128)S(1)} async-done(((f32[4,288,128]{2,1,0:T(8,128)}), f32[4,288,128]{2,1,0:T(8,128)S(1)}, u32[]{:S(2)}, u32[]{:S(2)}) %all-to-all-start.1) | async-done | bytes 589856 | tf_op jit(solution)/shard_map/all_to_all | solution.py:471
  67.8 0.0 copy-start.1
  67.8 3.5 %shard_map.77 = (f32[24,256]{1,0:T(8,128)S(1)}, f32[32,1,128]{2,1,0:T(1,128)}) custom-call(s32[3]{0:T(128)S(1)} %pad_add_fusion.1.place, s32[1]{0:T(128)S(6)} %copy.8.counts, f32[4,288,128]{2,1,0:T(8,128)S(1)} %all-to-all-done.1.gathered, f32[640,128]{1,0:T(8,128)S(1)} %bitcast.9), custom_call_target="tpu_custom_call" | custom-call | flops 5000000 | bytes 1048576 | tf_op jit(solution)/shard_map/pallas_call | solution.py:406
  71.3 14.8 %all-to-all-start.2 = ((f32[32,1,128]{2,1,0:T(1,128)}), f32[32,1,128]{2,1,0:T(1,128)S(1)}, u32[]{:S(2)}, u32[]{:S(2)}) async-start(f32[32,1,128]{2,1,0:T(1,128)} %get-tuple-element.32), calls=%async_computation.2 | async-start | bytes 32768 | tf_op jit(solution)/shard_map/all_to_all | solution.py:481
  86.2 0.0 copy-done
  86.2 0.0 copy-done.1
  86.2 2.6 %shard_map.78 = f32[3,8,2048]{2,1,0:T(8,128)} custom-call(s32[3]{0:T(128)S(1)} %pad_add_fusion.edge, f32[3,8,2048]{2,1,0:T(8,128)S(1)} %copy-done, f32[8,2048]{1,0:T(8,128)S(1)} %copy-done.1, f32[3,8,2048]{2,1,0:T(8,128)S(1)} %get-tuple-element.20.rims, f32[48,1024]{1,0:T(8,128)S(1)} %get-tuple-element.21.s1, f32[24,512]{1,0:T(8,128)S(1)} %get-tuple-element.22.s2, ...), custom_call_target="tpu_custom_call" | custom-call | flops 10000000 | bytes 1048576 | tf_op jit(solution)/shard_map/pallas_call | solution.py:406
  88.8 4.3 %all-to-all-done.2.got = f32[32,1,128]{2,1,0:T(1,128)S(1)} async-done(((f32[32,1,128]{2,1,0:T(1,128)}), f32[32,1,128]{2,1,0:T(1,128)S(1)}, u32[]{:S(2)}, u32[]{:S(2)}) %all-to-all-start.2) | async-done | bytes 16416 | tf_op jit(solution)/shard_map/all_to_all | solution.py:481
  93.1 1.4 %shard_map.79 = (f32[3]{0:T(128)}, f32[1,2]{1,0:T(1,128)}, f32[2]{0:T(128)}) custom-call(s32[3]{0:T(128)S(1)} %pad_add_fusion.1.place, f32[32,1,128]{2,1,0:T(1,128)S(1)} %all-to-all-done.2.got), custom_call_target="tpu_custom_call" | custom-call | flops 1000 | bytes 1048576 | tf_op jit(solution)/shard_map/pallas_call | solution.py:406
Async XLA Ops:
  1.7 10.2 %collective-permute-start.1 = (f32[7,8,2048]{2,1,0:T(8,128)S(1)}, f32[7,8,2048]{2,1,0:T(8,128)S(1)}, u32[]{:S(2)}, u32[]{:S(2)}) collective-permute-start(f32[7,8,2048]{2,1,0:T(8,128)S(1)} %pad_maximum_fusion.here), channel_id=1, source_target_pairs={{0,1},{1,0},{2,3},{3,2},{4,5},{5,4},{6,7},{7,6},{8,9},{9,8},{10,11... | collective-permute-start | bytes 1376264 | tf_op jit(solution)/shard_map/ppermute | solution.py:430
  6.1 5.9 %collective-permute-start = (f32[7,8,2048]{2,1,0:T(8,128)S(1)}, f32[7,8,2048]{2,1,0:T(8,128)S(1)}, u32[]{:S(2)}, u32[]{:S(2)}) collective-permute-start(f32[7,8,2048]{2,1,0:T(8,128)S(1)} %pad_maximum_fusion.here), channel_id=1, source_target_pairs={{1,2},{2,1},{3,4},{4,3},{5,6},{6,5},{7,8},{8,7},{9,10},{10,9},{11,... | collective-permute-start | bytes 1376264 | tf_op jit(solution)/shard_map/ppermute | solution.py:429
  19.4 36.2 %all-to-all-start = ((f32[16,40,128]{2,1,0:T(8,128)}), f32[16,40,128]{2,1,0:T(8,128)S(1)}, u32[]{:S(2)}, u32[]{:S(2)}) async-start(f32[16,40,128]{2,1,0:T(8,128)} %get-tuple-element.25), calls=%async_computation | async-start | bytes 655360 | tf_op jit(solution)/shard_map/all_to_all | solution.py:457
  41.8 5.8 %collective-permute-start.2 = (f32[8,512]{1,0:T(8,128)S(1)}, f32[8,512]{1,0:T(8,128)S(1)}, u32[]{:S(2)}, u32[]{:S(2)}) collective-permute-start(f32[8,512]{1,0:T(8,128)S(1)} %get-tuple-element.26), channel_id=1, source_target_pairs={{0,1},{1,2},{2,3},{3,4},{4,5},{5,6},{6,7},{7,8},{8,9},{9,10},{10,1... | collective-permute-start | bytes 49160 | tf_op jit(solution)/shard_map/ppermute | solution.py:458
  45.1 9.7 %collective-permute-start.3 = (f32[8,512]{1,0:T(8,128)S(1)}, f32[8,512]{1,0:T(8,128)S(1)}, u32[]{:S(2)}, u32[]{:S(2)}) collective-permute-start(f32[8,512]{1,0:T(8,128)S(1)} %get-tuple-element.27), channel_id=1, source_target_pairs={{1,0},{2,1},{3,2},{4,3},{5,4},{6,5},{7,6},{8,7},{9,8},{10,9},{11,1... | collective-permute-start | bytes 49160 | tf_op jit(solution)/shard_map/ppermute | solution.py:459
  56.5 11.3 %all-to-all-start.1 = ((f32[4,288,128]{2,1,0:T(8,128)}), f32[4,288,128]{2,1,0:T(8,128)S(1)}, u32[]{:S(2)}, u32[]{:S(2)}) async-start(f32[4,288,128]{2,1,0:T(8,128)} %shard_map.76), calls=%async_computation.1 | async-start | bytes 1179648 | tf_op jit(solution)/shard_map/all_to_all | solution.py:471
  61.3 24.9 %copy-start = (f32[3,8,2048]{2,1,0:T(8,128)S(1)}, f32[3,8,2048]{2,1,0:T(8,128)}, u32[]{:S(2)}) copy-start(f32[3,8,2048]{2,1,0:T(8,128)} %here.1) | copy-start | bytes 589828
  67.8 18.3 %copy-start.1 = (f32[8,2048]{1,0:T(8,128)S(1)}, f32[8,2048]{1,0:T(8,128)}, u32[]{:S(2)}) copy-start(f32[8,2048]{1,0:T(8,128)} %g.1) | copy-start | bytes 196612
  71.3 21.8 %all-to-all-start.2 = ((f32[32,1,128]{2,1,0:T(1,128)}), f32[32,1,128]{2,1,0:T(1,128)S(1)}, u32[]{:S(2)}, u32[]{:S(2)}) async-start(f32[32,1,128]{2,1,0:T(1,128)} %get-tuple-element.32), calls=%async_computation.2 | async-start | bytes 32768 | tf_op jit(solution)/shard_map/all_to_all | solution.py:481

commit v4 on v3

--- a/solution.py
+++ b/solution.py
@@ -142,7 +142,7 @@
 
 def down_kernel(
     edge, here, one, two,
-    packed, rims, s1_out, s2_out, k1_out, k2_out, to_below, to_above,
+    packed, rims, s1_out, s2_out, k1_out, k2_out, to_far, to_near,
     scratch, even, odd, parts,
 ):
     quarter = pair_matrix((256, 128), 0, 0.25)
@@ -201,11 +201,12 @@
             s1_out[...], k1_out[...] = s[:kept], k[:kept]
         else:
             s2_out[...], k2_out[...] = s[:kept], k[:kept]
-            to_below[...] = jnp.zeros_like(to_below)
-            to_above[...] = jnp.zeros_like(to_above)
+            to_far[...] = jnp.zeros_like(to_far)
+            to_near[...] = jnp.zeros_like(to_near)
             for slot in range(slots):
-                to_below[slot : slot + 1, :] = us[slot * 8 + 2 : slot * 8 + 3] * 16.0
-                to_above[slot : slot + 1, :] = us[slot * 8 + 3 : slot * 8 + 4] * 16.0
+                upper, lower = us[slot * 8 + 2 : slot * 8 + 3] * 16.0, us[slot * 8 + 3 : slot * 8 + 4] * 16.0
+                to_far[slot : slot + 1, :] = jnp.where(flip, upper, lower)
+                to_near[slot : slot + 1, :] = jnp.where(flip, lower, upper)
         level = [halve(x, scratch.at[q], quarter) for q, x in enumerate((k, rs, rw))]
 
     for q, x in enumerate(level):
@@ -243,7 +244,7 @@
             wide[x, start : start + rows, :] = lines[pl.ds(line, rows, stride=LINES), :]
 
 
-def coarse_kernel(place, counts, gathered, lines, e3, message, scratch, whole, *, fields, slabs, rows, cells):
+def coarse_kernel(place, gathered, lines, e3, message, scratch, whole, *, fields, slabs, rows, cells):
     slots = fields // 2
     quarter = pair_matrix((256, 128), 0, 0.25)
     spread = pair_matrix((128, 256), 1, 1.0)
@@ -285,7 +286,7 @@
     whole[8 + slots * n :, :] = jnp.zeros((8, 256), F32)
 
     lane = iota((1, 128), 1)
-    block = pl.multiple_of(place[1] * rows, 8)
+    block = pl.multiple_of(place[5] * rows, 8)
 
     def weighed(f):
         v = whole[pl.ds(8 + f * n + block, rows), :]
@@ -297,12 +298,12 @@
     for f in range(slots):
         total = total + jnp.where(lane == f, 64.0 * jnp.sum(weighed(f)), 0.0)
     other = field(2, slots) * v3[slots * n :]
-    total = total - jnp.where((lane == place[1]) & (lane < slots), 64.0 * jnp.sum(other), 0.0)
-    sent = jnp.where(lane < slots, total / cells, jnp.where(lane == slots, counts[0].astype(F32), 0.0))
+    total = total - jnp.where((lane == place[5]) & (lane < slots), 64.0 * jnp.sum(other), 0.0)
+    sent = jnp.where(lane < slots, total / cells, jnp.where(lane == slots, place[7].astype(F32), 0.0))
     for i in range(message.shape[0]):
         message[i] = sent
 
-    me = place[0]
+    me = place[4]
     e3[...] = jnp.zeros_like(e3)
     for f in range(slots):
         for r in range(3):
@@ -314,9 +315,9 @@
             e3[f * 8 + r : f * 8 + r + 1, :] = line
 
 
-def up_kernel(edge, here, g, rims, s1, s2, k1, k2, e3, top, bottom, out, scratch):
+def up_kernel(edge, here, rims, s1, s2, k1, k2, e3, far, near, out, scratch):
     spread = pair_matrix((128, 256), 1, 1.0)
-    slots = here.shape[0]
+    slots = out.shape[0]
 
     def relaxed(k, s, e, depth, window, swap):
         half, fr, fd, diag = faces(k, k.shape[1], None)
@@ -331,7 +332,9 @@
 
     def rimmed(v):
         row = iota(v.shape, 0) % 8
-        return jnp.where(row == 0, stacked(top, 8), jnp.where(row == 5, stacked(bottom, 8), v))
+        flip = edge[2] == 1
+        a, b = stacked(far, 8), stacked(near, 8)
+        return jnp.where(row == 0, jnp.where(flip, b, a), jnp.where(row == 5, jnp.where(flip, a, b), v))
 
     e = double_rows(double_cols(e3[...], spread), scratch)
     e = jnp.concatenate([e[f * 16 : f * 16 + 8] for f in range(slots)], axis=0)
@@ -339,7 +342,7 @@
     e = double_rows(double_cols(e, spread), scratch)
     e = relaxed(k1[...], s1[...], e, 1, 16, lambda v: v)
     e = double_cols(e, spread)
-    g = g[...]
+    g = here[2 * slots]
     row = iota(g.shape, 0)
     cols = g.shape[1]
 
@@ -384,7 +387,7 @@
     both = jnp.where(lane == 0, mean, jnp.where(lane == 1, var, 0.0))
     sums = jnp.where(lane == 0, mean, jnp.where(lane == 1, var / counted, 0.0))
     sums = jnp.sum(sums, axis=0, keepdims=True)
-    mine = row == place[2]
+    mine = row == place[6]
     own = jnp.sum(jnp.where(mine, table, 0.0), axis=0, keepdims=True)
     both = jnp.sum(jnp.where(mine, both, 0.0), axis=0, keepdims=True)
     for i in range(slots):
@@ -421,17 +424,16 @@
     levels = lax.axis_size("level")
     slabs = outer * inner
     me = lax.axis_index(SLAB)
-    from_above = [(i, i + 1) for i in range(slabs - 1)]
-    from_below = [(i + 1, i) for i in range(slabs - 1)]
     here = jnp.concatenate([coef_fine, coef_coarse, rhs_field[None]], axis=0)
     odd_down = [pair for i in range(1, slabs - 1, 2) for pair in ((i, i + 1), (i + 1, i))]
     odd_up = [pair for i in range(0, slabs, 2) for pair in ((i, i + 1), (i + 1, i))]
     one = lax.ppermute(here, SLAB, odd_down)
     two = lax.ppermute(here, SLAB, odd_up)
-    edge = jnp.stack([jnp.where(me == 0, 8, 0), jnp.where(me == slabs - 1, 16, 24), me % 2]).astype(jnp.int32)
-    place = jnp.stack([me, lax.axis_index("slab_0"), lax.axis_index("level")]).astype(jnp.int32)
-
-    packed, rims, s1, s2, k1, k2, to_below, to_above = call(
+    x, z, level = [lax.axis_index(axis) for axis in ("slab_0", "slab_1", "level")]
+    spot = [jnp.where(me == 0, 8, 0), jnp.where(me == slabs - 1, 16, 24), me % 2, z, me, x, level, level_counts[0]]
+    edge = jnp.stack([jnp.asarray(value, jnp.int32) for value in spot])
+
+    packed, rims, s1, s2, k1, k2, to_far, to_near = call(
         down_kernel,
         [
             shape(inner, LINES, 128),
@@ -455,9 +457,9 @@
         28,
     )
     lines = lax.all_to_all(packed, "slab_1", 0, 0, tiled=True)
-    top = lax.ppermute(to_below, SLAB, from_above)
-    bottom = lax.ppermute(to_above, SLAB, from_below)
-    lines, top, bottom = lax.optimization_barrier((lines, top, bottom))
+    far = lax.ppermute(to_far, SLAB, odd_down)
+    near = lax.ppermute(to_near, SLAB, odd_up)
+    lines, far, near = lax.optimization_barrier((lines, far, near))
     lines = lines.reshape(inner * LINES, 128)
     (wide,) = call(
         functools.partial(fan_kernel, fields=fields),
@@ -472,7 +474,7 @@
     e3, message = call(
         functools.partial(coarse_kernel, fields=fields, slabs=slabs, rows=inner, cells=float(rows * slabs * cols)),
         [shape(slots * 8, 256), shape(levels * outer, 1, 128)],
-        [place, level_counts],
+        [edge],
         [gathered, lines],
         [(2, 2 * (slots + 1) * slabs, 128), (slots * slabs + 16, 256)],
         5_000_000,
@@ -483,7 +485,7 @@
         up_kernel,
         [shape(slots, rows, cols)],
         [edge],
-        [coef_fine, rhs_field, rims, s1, s2, k1, k2, e3, top, bottom],
+        [here, rims, s1, s2, k1, k2, e3, far, near],
         [(cols // 2, 128)],
         10_000_000,
         16,
@@ -491,7 +493,7 @@
     diffs, moments, estimate = call(
         functools.partial(final_kernel, levels=levels, outer=outer),
         [shape(slots), shape(1, 2), shape(2)],
-        [place],
+        [edge],
         [got],
         [],
         1_000,

time: 94.9 us -> 93.9 us (0.989)
  blocking collectives: 0 us -> 11.1 us
  waiting for transfers between devices: 25.2 us -> 16.2 us
  starting transfers between devices: 50.8 us -> 48.6 us
    all_to_all x0 -> x1, blocking collectives: none -> 11.1 us  [on_device(): gathered = lax.all_to_all(wide, 'slab_0', 0, 0, tiled=True)]
    all_to_all x1 -> x0, waiting for transfers between devices: 6.55 us -> none  [on_device(): gathered = lax.all_to_all(wide, 'slab_0', 0, 0, tiled=True)]
    all_to_all x1 -> x0, starting transfers between devices: 4.02 us -> none  [on_device(): gathered = lax.all_to_all(wide, 'slab_0', 0, 0, tiled=True)]
    ppermute x2, waiting for transfers between devices: 8.4 us -> 6.59 us  [the longest x1 6.59 us: on_device(): near = lax.ppermute(to_near, SLAB, odd_up)]
    ppermute x2, starting transfers between devices: 4.55 us -> 6.35 us  [the longest x1 5.69 us: on_device(): near = lax.ppermute(to_near, SLAB, odd_up)]
  transfers between devices with their start and end apart: 7 -> 6, of which waited for: 6 -> 4; matrix products, arithmetic and copies ran while one was open for 0% -> 0% of each run, Pallas kernels for 3% -> 3%
where the time goes in v4:
time: 93.9 us; the launch traced here: 93.5 us
  starting transfers between devices  48.6 us (52%)
  waiting for transfers between devices  16.2 us (17%)
  Pallas kernels  15.1 us (16%)
  blocking collectives  11.1 us (12%)
  between operations  1.37 us (1%)
  other arithmetic  1.09 us (1%)
    all_to_all x1, starting transfers between devices, on_device(): lines = lax.all_to_all(packed, 'slab_1', 0, 0, tiled=True)  22.4 us
    pallas_call x5, Pallas kernels, call(): pl.pallas_call(kernel, out_shape=outs, in_specs=[SMEM] * len(smem) + [VME...  15.1 us
    all_to_all x1, starting transfers between devices, on_device(): got = lax.all_to_all(message, ('level', 'slab_0'), 0, 0, tiled=True)  14.8 us
    all_to_all x1, blocking collectives, on_device(): gathered = lax.all_to_all(wide, 'slab_0', 0, 0, tiled=True)  11.1 us
    ppermute x1, waiting for transfers between devices, on_device(): near = lax.ppermute(to_near, SLAB, odd_up)  6.59 us
    ppermute x1, starting transfers between devices, on_device(): near = lax.ppermute(to_near, SLAB, odd_up)  5.69 us
    ppermute x1, waiting for transfers between devices, on_device(): two = lax.ppermute(here, SLAB, odd_up)  4.4 us
    ppermute x1, starting transfers between devices, on_device(): two = lax.ppermute(here, SLAB, odd_up)  4.36 us
  transfers between devices with their start and end apart: 6, of which 4 were waited for; matrix products, arithmetic and copies ran while one was open for 0% of the time, Pallas kernels for 3%

profile of v4, /device:TPU:1, one launch (start us, length us, event | category | flops | bytes accessed | tf_op | source)
XLA Modules:
  0.0 93.5 jit_solution(8564643264781151035)
XLA Ops:
  0.6 1.1 %pad_maximum_fusion.here = f32[7,8,2048]{2,1,0:T(8,128)S(1)} fusion(f32[1,8,2048]{2,1,0:T(8,128)} %bitcast.11, f32[3,8,2048]{2,1,0:T(8,128)} %param.5, f32[3,8,2048]{2,1,0:T(8,128)} %param.4), kind=kLoop, calls=%fused_computation | loop fusion | flops 229376 | bytes 917504 | tf_op jit(solution)/shard_map/concatenate | solution.py:427
  1.7 4.4 %collective-permute-start.1 = (f32[7,8,2048]{2,1,0:T(8,128)S(1)}, f32[7,8,2048]{2,1,0:T(8,128)S(1)}, u32[]{:S(2)}, u32[]{:S(2)}) collective-permute-start(f32[7,8,2048]{2,1,0:T(8,128)S(1)} %pad_maximum_fusion.here), channel_id=1, source_target_pairs={{0,1},{1,0},{2,3},{3,2},{4,5},{5,4},{6,7},{7,6},{8,9},{9,8},{10,11... | collective-permute-start | bytes 1376264 | tf_op jit(solution)/shard_map/ppermute | solution.py:431
  6.1 0.7 collective-permute-start
  7.5 0.1 stack.31.edge.place
  7.5 4.4 %collective-permute-done.1.two = f32[7,8,2048]{2,1,0:T(8,128)S(1)} collective-permute-done((f32[7,8,2048]{2,1,0:T(8,128)S(1)}, f32[7,8,2048]{2,1,0:T(8,128)S(1)}, u32[]{:S(2)}, u32[]{:S(2)}) %collective-permute-start.1) | collective-permute-done | bytes 458784 | tf_op jit(solution)/shard_map/ppermute | solution.py:431
  12.0 0.0 collective-permute-done.one
  12.0 7.5 %shard_map.75 = (f32[16,40,128]{2,1,0:T(8,128)}, f32[3,8,2048]{2,1,0:T(8,128)S(1)}, f32[48,1024]{1,0:T(8,128)S(1)}, f32[24,512]{1,0:T(8,128)S(1)}, f32[48,1024]{...) custom-call(s32[8]{0:T(128)S(1)} %stack.31.edge.place, ...), custom_call_target="tpu_custom_call" | custom-call | flops 20000000 | bytes 1048576 | tf_op jit(solution)/shard_map/pallas_call | solution.py:409
  19.4 22.4 %all-to-all-start = ((f32[16,40,128]{2,1,0:T(8,128)}), f32[16,40,128]{2,1,0:T(8,128)S(1)}, u32[]{:S(2)}, u32[]{:S(2)}) async-start(f32[16,40,128]{2,1,0:T(8,128)} %get-tuple-element.25), calls=%async_computation | async-start | bytes 655360 | tf_op jit(solution)/shard_map/all_to_all | solution.py:459
  41.8 0.7 collective-permute-start.2
  42.5 5.7 %collective-permute-start.3 = (f32[8,512]{1,0:T(8,128)S(1)}, f32[8,512]{1,0:T(8,128)S(1)}, u32[]{:S(2)}, u32[]{:S(2)}) collective-permute-start(f32[8,512]{1,0:T(8,128)S(1)} %get-tuple-element.27), channel_id=1, source_target_pairs={{0,1},{1,0},{2,3},{3,2},{4,5},{5,4},{6,7},{7,6},{8,9},{9,8},{10,11... | collective-permute-start | bytes 49160 | tf_op jit(solution)/shard_map/ppermute | solution.py:461
  48.2 0.0 collective-permute-done.2.far
  48.2 6.6 %collective-permute-done.3.near = f32[8,512]{1,0:T(8,128)S(1)} collective-permute-done((f32[8,512]{1,0:T(8,128)S(1)}, f32[8,512]{1,0:T(8,128)S(1)}, u32[]{:S(2)}, u32[]{:S(2)}) %collective-permute-start.3) | collective-permute-done | bytes 16416 | tf_op jit(solution)/shard_map/ppermute | solution.py:461
  54.8 0.9 all-to-all-done
  55.6 0.1 shard_map.76
  55.7 11.1 %all_to_all.15.gathered = f32[4,288,128]{2,1,0:T(8,128)S(1)} all-to-all(f32[4,288,128]{2,1,0:T(8,128)S(1)} %shard_map.76), channel_id=1, replica_groups=mesh['level'=8,'slab_0'=4,'slab_1'=16] {'slab_0'}, dimensions={0} | all-to-all | bytes 1179648 | tf_op jit(solution)/shard_map/all_to_all | solution.py:473
  66.8 3.5 %shard_map.77 = (f32[24,256]{1,0:T(8,128)S(1)}, f32[32,1,128]{2,1,0:T(1,128)}) custom-call(s32[8]{0:T(128)S(1)} %stack.31.edge.place, f32[4,288,128]{2,1,0:T(8,128)S(1)} %all_to_all.15.gathered, f32[640,128]{1,0:T(8,128)S(1)} %bitcast.10), custom_call_target="tpu_custom_call" | custom-call | flops 5000000 | bytes 1048576 | tf_op jit(solution)/shard_map/pallas_call | solution.py:409
  70.3 14.8 %all-to-all-start.2 = ((f32[32,1,128]{2,1,0:T(1,128)}), f32[32,1,128]{2,1,0:T(1,128)S(1)}, u32[]{:S(2)}, u32[]{:S(2)}) async-start(f32[32,1,128]{2,1,0:T(1,128)} %get-tuple-element.32), calls=%async_computation.2 | async-start | bytes 32768 | tf_op jit(solution)/shard_map/all_to_all | solution.py:483
  85.1 2.6 %shard_map.78 = f32[3,8,2048]{2,1,0:T(8,128)} custom-call(s32[8]{0:T(128)S(1)} %stack.31.edge.place, f32[7,8,2048]{2,1,0:T(8,128)S(1)} %pad_maximum_fusion.here, f32[3,8,2048]{2,1,0:T(8,128)S(1)} %get-tuple-element.20.rims, f32[48,1024]{1,0:T(8,128)S(1)} %get-tuple-element.21.s1, f32[24,512]{1,0:T(8,128)S(1)} %get-tuple-element.22.s2, ...), custom_call_target="tpu_custom_call" | custom-call | flops 10000000 | bytes 1048576 | tf_op jit(solution)/shard_map/pallas_call | solution.py:409
  87.7 4.4 %all-to-all-done.2.got = f32[32,1,128]{2,1,0:T(1,128)S(1)} async-done(((f32[32,1,128]{2,1,0:T(1,128)}), f32[32,1,128]{2,1,0:T(1,128)S(1)}, u32[]{:S(2)}, u32[]{:S(2)}) %all-to-all-start.2) | async-done | bytes 16416 | tf_op jit(solution)/shard_map/all_to_all | solution.py:483
  92.1 1.4 %shard_map.79 = (f32[3]{0:T(128)}, f32[1,2]{1,0:T(1,128)}, f32[2]{0:T(128)}) custom-call(s32[8]{0:T(128)S(1)} %stack.31.edge.place, f32[32,1,128]{2,1,0:T(1,128)S(1)} %all-to-all-done.2.got), custom_call_target="tpu_custom_call" | custom-call | flops 1000 | bytes 1048576 | tf_op jit(solution)/shard_map/pallas_call | solution.py:409
Async XLA Ops:
  1.7 10.2 %collective-permute-start.1 = (f32[7,8,2048]{2,1,0:T(8,128)S(1)}, f32[7,8,2048]{2,1,0:T(8,128)S(1)}, u32[]{:S(2)}, u32[]{:S(2)}) collective-permute-start(f32[7,8,2048]{2,1,0:T(8,128)S(1)} %pad_maximum_fusion.here), channel_id=1, source_target_pairs={{0,1},{1,0},{2,3},{3,2},{4,5},{5,4},{6,7},{7,6},{8,9},{9,8},{10,11... | collective-permute-start | bytes 1376264 | tf_op jit(solution)/shard_map/ppermute | solution.py:431
  6.1 5.9 %collective-permute-start = (f32[7,8,2048]{2,1,0:T(8,128)S(1)}, f32[7,8,2048]{2,1,0:T(8,128)S(1)}, u32[]{:S(2)}, u32[]{:S(2)}) collective-permute-start(f32[7,8,2048]{2,1,0:T(8,128)S(1)} %pad_maximum_fusion.here), channel_id=1, source_target_pairs={{1,2},{2,1},{3,4},{4,3},{5,6},{6,5},{7,8},{8,7},{9,10},{10,9},{11,... | collective-permute-start | bytes 1376264 | tf_op jit(solution)/shard_map/ppermute | solution.py:430
  19.4 36.2 %all-to-all-start = ((f32[16,40,128]{2,1,0:T(8,128)}), f32[16,40,128]{2,1,0:T(8,128)S(1)}, u32[]{:S(2)}, u32[]{:S(2)}) async-start(f32[16,40,128]{2,1,0:T(8,128)} %get-tuple-element.25), calls=%async_computation | async-start | bytes 655360 | tf_op jit(solution)/shard_map/all_to_all | solution.py:459
  41.8 6.4 %collective-permute-start.2 = (f32[8,512]{1,0:T(8,128)S(1)}, f32[8,512]{1,0:T(8,128)S(1)}, u32[]{:S(2)}, u32[]{:S(2)}) collective-permute-start(f32[8,512]{1,0:T(8,128)S(1)} %get-tuple-element.26), channel_id=1, source_target_pairs={{1,2},{2,1},{3,4},{4,3},{5,6},{6,5},{7,8},{8,7},{9,10},{10,9},{11,... | collective-permute-start | bytes 49160 | tf_op jit(solution)/shard_map/ppermute | solution.py:460
  42.5 12.3 %collective-permute-start.3 = (f32[8,512]{1,0:T(8,128)S(1)}, f32[8,512]{1,0:T(8,128)S(1)}, u32[]{:S(2)}, u32[]{:S(2)}) collective-permute-start(f32[8,512]{1,0:T(8,128)S(1)} %get-tuple-element.27), channel_id=1, source_target_pairs={{0,1},{1,0},{2,3},{3,2},{4,5},{5,4},{6,7},{7,6},{8,9},{9,8},{10,11... | collective-permute-start | bytes 49160 | tf_op jit(solution)/shard_map/ppermute | solution.py:461
  70.3 21.8 %all-to-all-start.2 = ((f32[32,1,128]{2,1,0:T(1,128)}), f32[32,1,128]{2,1,0:T(1,128)S(1)}, u32[]{:S(2)}, u32[]{:S(2)}) async-start(f32[32,1,128]{2,1,0:T(1,128)} %get-tuple-element.32), calls=%async_computation.2 | async-start | bytes 32768 | tf_op jit(solution)/shard_map/all_to_all | solution.py:483

commit v5 on v4

--- a/solution.py
+++ b/solution.py
@@ -73,8 +73,9 @@
     rest = a - high.astype(F32)
     middle = rest.astype(jnp.bfloat16)
     low = (rest - middle.astype(F32)).astype(jnp.bfloat16)
-    one = functools.partial(jnp.dot, preferred_element_type=F32)
-    return one(high, b) + (one(middle, b) + one(low, b))
+    rows = a.shape[0]
+    got = jnp.dot(jnp.concatenate([high, middle, low], axis=0), b, preferred_element_type=F32)
+    return got[:rows] + (got[rows : 2 * rows] + got[2 * rows :])
 
 
 def pieces(x, width=128):

time: 93.9 us -> 93.7 us (level)
  no operation moved by 1% of the time
where the time goes in v5:
time: 93.7 us; the launch traced here: 93.4 us
  starting transfers between devices  48.6 us (52%)
  waiting for transfers between devices  16.3 us (17%)
  Pallas kernels  14.8 us (16%)
  blocking collectives  11.1 us (12%)
  between operations  1.37 us (1%)
  other arithmetic  1.09 us (1%)
    all_to_all x1, starting transfers between devices, on_device(): lines = lax.all_to_all(packed, 'slab_1', 0, 0, tiled=True)  22.4 us
    pallas_call x5, Pallas kernels, call(): pl.pallas_call(kernel, out_shape=outs, in_specs=[SMEM] * len(smem) + [VME...  14.8 us
    all_to_all x1, starting transfers between devices, on_device(): got = lax.all_to_all(message, ('level', 'slab_0'), 0, 0, tiled=True)  14.8 us
    all_to_all x1, blocking collectives, on_device(): gathered = lax.all_to_all(wide, 'slab_0', 0, 0, tiled=True)  11.1 us
    ppermute x1, waiting for transfers between devices, on_device(): near = lax.ppermute(to_near, SLAB, odd_up)  6.59 us
    ppermute x1, starting transfers between devices, on_device(): near = lax.ppermute(to_near, SLAB, odd_up)  5.69 us
    all_to_all x1, waiting for transfers between devices, on_device(): got = lax.all_to_all(message, ('level', 'slab_0'), 0, 0, tiled=True)  4.44 us
    ppermute x1, waiting for transfers between devices, on_device(): two = lax.ppermute(here, SLAB, odd_up)  4.4 us
  transfers between devices with their start and end apart: 6, of which 4 were waited for; matrix products, arithmetic and copies ran while one was open for 0% of the time, Pallas kernels for 3%

profile of v5, /device:TPU:1, one launch (start us, length us, event | category | flops | bytes accessed | tf_op | source)
XLA Modules:
  0.0 93.4 jit_solution(18314826618954837757)
XLA Ops:
  0.6 1.1 %pad_maximum_fusion.here = f32[7,8,2048]{2,1,0:T(8,128)S(1)} fusion(f32[1,8,2048]{2,1,0:T(8,128)} %bitcast.11, f32[3,8,2048]{2,1,0:T(8,128)} %param.5, f32[3,8,2048]{2,1,0:T(8,128)} %param.4), kind=kLoop, calls=%fused_computation | loop fusion | flops 229376 | bytes 917504 | tf_op jit(solution)/shard_map/concatenate | solution.py:428
  1.7 4.4 %collective-permute-start.1 = (f32[7,8,2048]{2,1,0:T(8,128)S(1)}, f32[7,8,2048]{2,1,0:T(8,128)S(1)}, u32[]{:S(2)}, u32[]{:S(2)}) collective-permute-start(f32[7,8,2048]{2,1,0:T(8,128)S(1)} %pad_maximum_fusion.here), channel_id=1, source_target_pairs={{0,1},{1,0},{2,3},{3,2},{4,5},{5,4},{6,7},{7,6},{8,9},{9,8},{10,11... | collective-permute-start | bytes 1376264 | tf_op jit(solution)/shard_map/ppermute | solution.py:432
  6.1 0.7 collective-permute-start
  7.5 0.1 stack.31.edge.place
  7.5 4.4 %collective-permute-done.1.two = f32[7,8,2048]{2,1,0:T(8,128)S(1)} collective-permute-done((f32[7,8,2048]{2,1,0:T(8,128)S(1)}, f32[7,8,2048]{2,1,0:T(8,128)S(1)}, u32[]{:S(2)}, u32[]{:S(2)}) %collective-permute-start.1) | collective-permute-done | bytes 458784 | tf_op jit(solution)/shard_map/ppermute | solution.py:432
  12.0 0.0 collective-permute-done.one
  12.0 7.4 %shard_map.75 = (f32[16,40,128]{2,1,0:T(8,128)}, f32[3,8,2048]{2,1,0:T(8,128)S(1)}, f32[48,1024]{1,0:T(8,128)S(1)}, f32[24,512]{1,0:T(8,128)S(1)}, f32[48,1024]{...) custom-call(s32[8]{0:T(128)S(1)} %stack.31.edge.place, ...), custom_call_target="tpu_custom_call" | custom-call | flops 20000000 | bytes 1048576 | tf_op jit(solution)/shard_map/pallas_call | solution.py:410
  19.3 22.4 %all-to-all-start = ((f32[16,40,128]{2,1,0:T(8,128)}), f32[16,40,128]{2,1,0:T(8,128)S(1)}, u32[]{:S(2)}, u32[]{:S(2)}) async-start(f32[16,40,128]{2,1,0:T(8,128)} %get-tuple-element.25), calls=%async_computation | async-start | bytes 655360 | tf_op jit(solution)/shard_map/all_to_all | solution.py:460
  41.7 0.7 collective-permute-start.2
  42.4 5.7 %collective-permute-start.3 = (f32[8,512]{1,0:T(8,128)S(1)}, f32[8,512]{1,0:T(8,128)S(1)}, u32[]{:S(2)}, u32[]{:S(2)}) collective-permute-start(f32[8,512]{1,0:T(8,128)S(1)} %get-tuple-element.27), channel_id=1, source_target_pairs={{0,1},{1,0},{2,3},{3,2},{4,5},{5,4},{6,7},{7,6},{8,9},{9,8},{10,11... | collective-permute-start | bytes 49160 | tf_op jit(solution)/shard_map/ppermute | solution.py:462
  48.1 0.0 collective-permute-done.2.far
  48.1 6.6 %collective-permute-done.3.near = f32[8,512]{1,0:T(8,128)S(1)} collective-permute-done((f32[8,512]{1,0:T(8,128)S(1)}, f32[8,512]{1,0:T(8,128)S(1)}, u32[]{:S(2)}, u32[]{:S(2)}) %collective-permute-start.3) | collective-permute-done | bytes 16416 | tf_op jit(solution)/shard_map/ppermute | solution.py:462
  54.7 0.9 all-to-all-done
  55.5 0.1 shard_map.76
  55.6 11.1 %all_to_all.15.gathered = f32[4,288,128]{2,1,0:T(8,128)S(1)} all-to-all(f32[4,288,128]{2,1,0:T(8,128)S(1)} %shard_map.76), channel_id=1, replica_groups=mesh['level'=8,'slab_0'=4,'slab_1'=16] {'slab_0'}, dimensions={0} | all-to-all | bytes 1179648 | tf_op jit(solution)/shard_map/all_to_all | solution.py:474
  66.7 3.5 %shard_map.77 = (f32[24,256]{1,0:T(8,128)S(1)}, f32[32,1,128]{2,1,0:T(1,128)}) custom-call(s32[8]{0:T(128)S(1)} %stack.31.edge.place, f32[4,288,128]{2,1,0:T(8,128)S(1)} %all_to_all.15.gathered, f32[640,128]{1,0:T(8,128)S(1)} %bitcast.10), custom_call_target="tpu_custom_call" | custom-call | flops 5000000 | bytes 1048576 | tf_op jit(solution)/shard_map/pallas_call | solution.py:410
  70.2 14.8 %all-to-all-start.2 = ((f32[32,1,128]{2,1,0:T(1,128)}), f32[32,1,128]{2,1,0:T(1,128)S(1)}, u32[]{:S(2)}, u32[]{:S(2)}) async-start(f32[32,1,128]{2,1,0:T(1,128)} %get-tuple-element.32), calls=%async_computation.2 | async-start | bytes 32768 | tf_op jit(solution)/shard_map/all_to_all | solution.py:484
  85.0 2.5 %shard_map.78 = f32[3,8,2048]{2,1,0:T(8,128)} custom-call(s32[8]{0:T(128)S(1)} %stack.31.edge.place, f32[7,8,2048]{2,1,0:T(8,128)S(1)} %pad_maximum_fusion.here, f32[3,8,2048]{2,1,0:T(8,128)S(1)} %get-tuple-element.20.rims, f32[48,1024]{1,0:T(8,128)S(1)} %get-tuple-element.21.s1, f32[24,512]{1,0:T(8,128)S(1)} %get-tuple-element.22.s2, ...), custom_call_target="tpu_custom_call" | custom-call | flops 10000000 | bytes 1048576 | tf_op jit(solution)/shard_map/pallas_call | solution.py:410
  87.5 4.4 %all-to-all-done.2.got = f32[32,1,128]{2,1,0:T(1,128)S(1)} async-done(((f32[32,1,128]{2,1,0:T(1,128)}), f32[32,1,128]{2,1,0:T(1,128)S(1)}, u32[]{:S(2)}, u32[]{:S(2)}) %all-to-all-start.2) | async-done | bytes 16416 | tf_op jit(solution)/shard_map/all_to_all | solution.py:484
  91.9 1.4 %shard_map.79 = (f32[3]{0:T(128)}, f32[1,2]{1,0:T(1,128)}, f32[2]{0:T(128)}) custom-call(s32[8]{0:T(128)S(1)} %stack.31.edge.place, f32[32,1,128]{2,1,0:T(1,128)S(1)} %all-to-all-done.2.got), custom_call_target="tpu_custom_call" | custom-call | flops 1000 | bytes 1048576 | tf_op jit(solution)/shard_map/pallas_call | solution.py:410
Async XLA Ops:
  1.7 10.2 %collective-permute-start.1 = (f32[7,8,2048]{2,1,0:T(8,128)S(1)}, f32[7,8,2048]{2,1,0:T(8,128)S(1)}, u32[]{:S(2)}, u32[]{:S(2)}) collective-permute-start(f32[7,8,2048]{2,1,0:T(8,128)S(1)} %pad_maximum_fusion.here), channel_id=1, source_target_pairs={{0,1},{1,0},{2,3},{3,2},{4,5},{5,4},{6,7},{7,6},{8,9},{9,8},{10,11... | collective-permute-start | bytes 1376264 | tf_op jit(solution)/shard_map/ppermute | solution.py:432
  6.1 5.9 %collective-permute-start = (f32[7,8,2048]{2,1,0:T(8,128)S(1)}, f32[7,8,2048]{2,1,0:T(8,128)S(1)}, u32[]{:S(2)}, u32[]{:S(2)}) collective-permute-start(f32[7,8,2048]{2,1,0:T(8,128)S(1)} %pad_maximum_fusion.here), channel_id=1, source_target_pairs={{1,2},{2,1},{3,4},{4,3},{5,6},{6,5},{7,8},{8,7},{9,10},{10,9},{11,... | collective-permute-start | bytes 1376264 | tf_op jit(solution)/shard_map/ppermute | solution.py:431
  19.3 36.2 %all-to-all-start = ((f32[16,40,128]{2,1,0:T(8,128)}), f32[16,40,128]{2,1,0:T(8,128)S(1)}, u32[]{:S(2)}, u32[]{:S(2)}) async-start(f32[16,40,128]{2,1,0:T(8,128)} %get-tuple-element.25), calls=%async_computation | async-start | bytes 655360 | tf_op jit(solution)/shard_map/all_to_all | solution.py:460
  41.7 6.4 %collective-permute-start.2 = (f32[8,512]{1,0:T(8,128)S(1)}, f32[8,512]{1,0:T(8,128)S(1)}, u32[]{:S(2)}, u32[]{:S(2)}) collective-permute-start(f32[8,512]{1,0:T(8,128)S(1)} %get-tuple-element.26), channel_id=1, source_target_pairs={{1,2},{2,1},{3,4},{4,3},{5,6},{6,5},{7,8},{8,7},{9,10},{10,9},{11,... | collective-permute-start | bytes 49160 | tf_op jit(solution)/shard_map/ppermute | solution.py:461
  42.4 12.3 %collective-permute-start.3 = (f32[8,512]{1,0:T(8,128)S(1)}, f32[8,512]{1,0:T(8,128)S(1)}, u32[]{:S(2)}, u32[]{:S(2)}) collective-permute-start(f32[8,512]{1,0:T(8,128)S(1)} %get-tuple-element.27), channel_id=1, source_target_pairs={{0,1},{1,0},{2,3},{3,2},{4,5},{5,4},{6,7},{7,6},{8,9},{9,8},{10,11... | collective-permute-start | bytes 49160 | tf_op jit(solution)/shard_map/ppermute | solution.py:462
  70.2 21.8 %all-to-all-start.2 = ((f32[32,1,128]{2,1,0:T(1,128)}), f32[32,1,128]{2,1,0:T(1,128)S(1)}, u32[]{:S(2)}, u32[]{:S(2)}) async-start(f32[32,1,128]{2,1,0:T(1,128)} %get-tuple-element.32), calls=%async_computation.2 | async-start | bytes 32768 | tf_op jit(solution)/shard_map/all_to_all | solution.py:484
